TPU v7x, 32 devices: a whole 2x2x4 slice. The times are simulated.
32 devices in a mesh: mem: 8 (over z, y), dom: 4 (over x, core).
Axes of the slice: x: 2, y: 2, z: 4, core: 2. Of those that a mesh axis runs over, the one named last changes fastest.
Arguments:
- particle_states: float32 [64, 3, 256, 1024], P('mem', None, 'dom'), may hold values from -6 to 6
- coriolis: float32 [256], replicated, may hold values from -0.6 to 0.6
- observed_cells: int32 [4, 64, 512], P('dom', 'mem'), may hold values from 0 to 1023
- observed_values: float32 [4, 64, 512], P('dom', 'mem'), may hold values from -6 to 15
- resample_draws: int32 [4, 64, 8, 192], P('dom', 'mem'), may hold values from 0 to 63
Outputs:
- analysed: float32 [64, 3, 256, 1024], P('mem', None, 'dom')
All inputs are finite; a program needn't handle non-finite values.
Results may differ from a plain program's by a relative error of at most 0.0003.
Values sent between devices are 32-bit elements; how exact they have to be, the bound alone decides.
No kernel may reach another device: no remote copies, remote signals or barrier semaphores. Data moves between devices by JAX's collectives and lax.ppermute only.
A program may use at most 128 MiB of HBM per device.

v0:
```python
import functools

import jax
import jax.numpy as jnp
from jax import lax
from jax.experimental import pallas as pl
from jax.experimental.pallas import tpu as pltpu
from jax.sharding import PartitionSpec as P


LBLK = 128
LOC = 64
STEPS = 2
SUBLANES = 8
LANES = 128
EARLY_MEMBERS = 3


FLOW_FACTOR = 1.0
PRESSURE_FACTOR = 1.0
OBSERVATION_VARIANCE = 16.0
RELAXATION = 0.5
MERGE_FIRST = 0.75
BLEND_COEF_TWO = (13.0**0.5 + 1.0) / 8.0
MERGE_THIRD = -(13.0**0.5 - 1.0) / 8.0


def edge_rows(array, axis, dim, width):
    count, length = (lax.axis_size(axis), array.shape[dim])
    up = [(i, i + 1) for i in range(count - 1)]
    down = [(j, i) for i, j in up]
    before = lax.ppermute(lax.slice_in_dim(array, length - width, length, axis=dim), axis, up)
    after = lax.ppermute(lax.slice_in_dim(array, 0, width, axis=dim), axis, down)
    return before, after


def early_kernel(margin, coriolis_ref, states_ref, all_ref, here, there):
    forecast_steps(margin, None, coriolis_ref, states_ref, None, None,
                   all_ref.at[:, 0], all_ref.at[:, 1:], here, there)


def forecast_steps(margin, inside_ref, coriolis_ref, states_ref, before_ref, after_ref,
                   height_ref, winds_ref, here, there):
    rows, width = states_ref.shape[2:]
    last = rows // SUBLANES + 2
    first_row = 2 * SUBLANES
    with_halo = before_ref is not None

    def tile(t, shift=0):
        return slice(t * SUBLANES + shift, (t + 1) * SUBLANES + shift)

    def east(quantity):
        return pltpu.roll(quantity, width - 1, 1) - pltpu.roll(quantity, 1, 1)

    def north(ref, field, t):
        return ref[field, tile(t, 1), :] - ref[field, tile(t, -1), :]

    def masked(quantity, t):
        if t == 1:
            return quantity * inside_ref[0]
        if t == last:
            return quantity * inside_ref[1]
        return quantity

    here[:, first_row : first_row + rows, :] = states_ref[0]
    if with_halo:
        here[:, first_row - margin : first_row, :] = before_ref[0]
        here[:, first_row + rows : first_row + rows + margin, :] = after_ref[0]
    old, new = here, there
    for step in range(STEPS):
        final = step == STEPS - 1
        for t in range(1, last + 1) if with_halo else range(2, last):
            slope = east(old[1, tile(t), :]) + north(old, 2, t)
            height = masked(old[0, tile(t), :] - (0.5 * FLOW_FACTOR) * slope, t)
            new[0, tile(t), :] = height
            if final and 1 < t < last:
                height_ref[0, tile(t - 2), :] = height
        for t in range(1, last + 1) if with_halo and not final else range(2, last):
            factor = jnp.concatenate([coriolis_ref[tile(t), :]] * (width // LANES), axis=1)
            east_old, north_old = old[1, tile(t), :], old[2, tile(t), :]
            east_new = (
                east_old - (0.5 * PRESSURE_FACTOR) * east(new[0, tile(t), :]) + factor * north_old
            )
            north_new = north_old - (0.5 * PRESSURE_FACTOR) * north(new, 0, t) - factor * east_old
            if final:
                winds_ref[0, 0, tile(t - 2), :] = east_new
                winds_ref[0, 1, tile(t - 2), :] = north_new
            else:
                new[1, tile(t), :] = masked(east_new, t)
                new[2, tile(t), :] = masked(north_new, t)
        old, new = new, old


def coriolis_frame(coriolis, band_index, rows):
    frame = rows + 4 * SUBLANES
    factors = lax.dynamic_slice_in_dim(
        jnp.pad(coriolis, (2 * SUBLANES, 2 * SUBLANES)), band_index * rows, frame
    )
    return jnp.broadcast_to(factors[:, None], (frame, LANES))


def forecast_cost(members, states):
    size = members * states.size // states.shape[0]
    return pl.CostEstimate(flops=40 * size * STEPS, bytes_accessed=8 * size, transcendentals=0)


def early_forecast(states, factors, early):
    fields, rows, width = states.shape[1:]
    return pl.pallas_call(
        functools.partial(early_kernel, 2 * STEPS),
        grid=(early,),
        in_specs=[
            pl.BlockSpec(factors.shape, lambda m: (0, 0)),
            pl.BlockSpec((1, fields, rows, width), lambda m: (m, 0, 0, 0)),
        ],
        out_specs=pl.BlockSpec((1, fields, rows, width), lambda m: (m, 0, 0, 0)),
        out_shape=jax.ShapeDtypeStruct((early, fields, rows, width), jnp.float32),
        scratch_shapes=[pltpu.VMEM((fields, factors.shape[0], width), jnp.float32)] * 2,
        cost_estimate=forecast_cost(early, states),
    )(factors, states)


def forecast(states, before, after, factors, band_index, band_count):
    members, fields, rows, width = states.shape
    margin = 2 * STEPS
    inside = jnp.stack([band_index > 0, band_index < band_count - 1]).astype(jnp.float32)
    return pl.pallas_call(
        functools.partial(forecast_steps, margin),
        grid=(members,),
        in_specs=[
            pl.BlockSpec(memory_space=pltpu.SMEM),
            pl.BlockSpec(factors.shape, lambda m: (0, 0)),
            pl.BlockSpec((1, fields, rows, width), lambda m: (m, 0, 0, 0)),
            pl.BlockSpec((1, fields, margin, width), lambda m: (m, 0, 0, 0)),
            pl.BlockSpec((1, fields, margin, width), lambda m: (m, 0, 0, 0)),
        ],
        out_specs=[
            pl.BlockSpec((1, rows, width), lambda m: (m, 0, 0)),
            pl.BlockSpec((1, fields - 1, rows, width), lambda m: (m, 0, 0, 0)),
        ],
        out_shape=[
            jax.ShapeDtypeStruct((members, rows, width), jnp.float32),
            jax.ShapeDtypeStruct((members, fields - 1, rows, width), jnp.float32),
        ],
        scratch_shapes=[pltpu.VMEM((fields, factors.shape[0], width), jnp.float32)] * 2,
        cost_estimate=forecast_cost(members, states),
    )(inside, factors, states, before, after)


def tapering(cells, grid_width, block_cells, length):
    longitude = cells.astype(jnp.float32)
    tile_total = grid_width // block_cells
    centre = jnp.arange(tile_total).astype(jnp.float32) * block_cells + 0.5 * (block_cells - 1)
    distance = jnp.abs(longitude[..., :, None] - centre)
    distance = jnp.minimum(distance, grid_width - distance)
    return jnp.exp(-0.5 * (distance / length) ** 2)


def member_weights(heights, cells, values, block_cells, length):
    grid_width = heights.shape[-1]
    chosen_cells = (
        cells[:, None, :] == lax.broadcasted_iota(jnp.int32, (1, grid_width, 1), 1)
    ).astype(jnp.float32)
    observed = jnp.einsum("erl,rlo->reo", heights, chosen_cells, precision=lax.Precision.HIGHEST)
    misfit = (values[:, None, :] - observed) ** 2
    taper_weights = tapering(cells, grid_width, block_cells, length)
    likelihood = (
        -0.5
        / OBSERVATION_VARIANCE
        * jnp.einsum("reo,rob->rbe", misfit, taper_weights, precision=lax.Precision.HIGHEST)
    )
    largest = jnp.max(likelihood, axis=-1, keepdims=True)
    scaled = jnp.exp(likelihood - largest)
    return scaled / jnp.sum(scaled, axis=-1, keepdims=True)


def mixing_matrix(weights, draws):
    member_count = weights.shape[-1]
    split = draws.reshape(draws.shape[:-1] + (3, member_count))
    column = lax.broadcasted_iota(jnp.int32, (1, 1, 1, member_count), 3)
    picks = MERGE_FIRST * (split[:, :, 0, :, None] == column).astype(jnp.float32)
    picks = picks + BLEND_COEF_TWO * (split[:, :, 1, :, None] == column).astype(jnp.float32)
    picks = picks + MERGE_THIRD * (split[:, :, 2, :, None] == column).astype(jnp.float32)
    return (1.0 - RELAXATION) * weights[:, :, None, :] + RELAXATION * picks


def merge_fields(members, mixing, block_cells):
    member_count, fields, count_of_rows, grid_width = members.shape
    blocks = members.reshape(
        member_count, fields, count_of_rows, grid_width // block_cells, block_cells
    )
    updated = jnp.einsum("rbek,kfrbc->efrbc", mixing, blocks, precision=lax.Precision.HIGHEST)
    return updated.reshape(member_count, fields, count_of_rows, grid_width)


def shifts(count, d, targets):
    return [(i, (i + d) % count) for i in range(count) if (i + d) % count in targets]


def send_all(pieces, axis, targets=None):
    count = lax.axis_size(axis)
    targets = range(count) if targets is None else targets
    return pieces[:1] + [
        lax.ppermute(pieces[d], axis, shifts(count, d, targets)) for d in range(1, count)
    ]


def row_pieces(array, axis, dim):
    count = lax.axis_size(axis)
    own = lax.axis_index(axis)
    length = array.shape[dim] // count
    pieces = [
        lax.dynamic_slice_in_dim(array, lax.rem(own + d, count) * length, length, axis=dim)
        for d in range(count)
    ]
    return lax.optimization_barrier(pieces)


def put_back(whole, received, axis, field):
    count = lax.axis_size(axis)
    own = lax.axis_index(axis)
    length = received[0].shape[2]
    for d, piece in enumerate(received):
        start = lax.rem(own + count - d, count) * length
        whole = lax.dynamic_update_slice(whole, piece, (0, field, start, 0))
    return whole


def relative_draws(draws, axis, members_dev, early):
    count = lax.axis_size(axis)
    own = lax.axis_index(axis)
    member = draws % members_dev
    distance = lax.rem(own + count - draws // members_dev, count)
    late = members_dev - early
    place = jnp.where(
        member < early,
        distance * early + member,
        count * early + distance * late + member - early,
    )
    split = place.reshape(place.shape[:-1] + (3, count, members_dev))
    doubled = jnp.concatenate([split, split], axis=-2)
    turned = lax.dynamic_slice_in_dim(doubled, own, count, axis=-2)
    return turned.reshape(draws.shape)


def body(particle_states, coriolis, observed_cells, observed_values, resample_draws):
    members_dev, _, count_of_rows, _ = particle_states.shape
    count = lax.axis_size("mem")
    own = lax.axis_index("mem")
    band_index = lax.axis_index("dom")
    margin = 2 * STEPS
    early = EARLY_MEMBERS
    piece = count_of_rows // count
    inner = [
        j for j in range(count)
        if j * piece >= margin and (j + 1) * piece <= count_of_rows - margin
    ]
    outer = [j for j in range(count) if j not in inner]
    factors = coriolis_frame(coriolis, band_index, count_of_rows)

    first = early_forecast(particle_states, factors, early)
    first_pieces = row_pieces(first, "mem", 2)
    first_inner = send_all(first_pieces, "mem", inner)
    states, _ = lax.optimization_barrier((particle_states, first_pieces))
    before, after = edge_rows(states, "dom", 2, margin)
    height, winds = forecast(states, before, after, factors, band_index, lax.axis_size("dom"))
    again = jnp.concatenate([height[:early, None], winds[:early]], axis=1)
    first_outer = send_all(row_pieces(again, "mem", 2), "mem", outer)
    late_heights = send_all(row_pieces(height[early:], "mem", 1), "mem")
    late_winds = send_all(row_pieces(winds[early:], "mem", 2), "mem")
    first_inner, first_outer, late_heights = lax.optimization_barrier(
        (first_inner, first_outer, late_heights)
    )

    is_outer = jnp.any(jnp.stack([own == j for j in outer]))
    firsts = [jnp.where(is_outer, a, b) for a, b in zip(first_outer, first_inner)]
    heights = jnp.concatenate([a[:, 0] for a in firsts] + late_heights, axis=0)
    winds_all = jnp.concatenate([a[:, 1:] for a in firsts] + late_winds, axis=0)

    cells = observed_cells[0]
    values = observed_values[0]
    draws = relative_draws(resample_draws[0], "mem", members_dev, early)
    weights = member_weights(heights, cells, values, LBLK, LOC)
    mixing = mixing_matrix(weights, draws)

    def hand_back(members):
        updated = merge_fields(members, mixing, LBLK)
        pieces = [updated[d * members_dev : (d + 1) * members_dev] for d in range(count)]
        return send_all(pieces, "mem")

    analysed = jnp.zeros(particle_states.shape, particle_states.dtype)
    analysed = put_back(analysed, hand_back(heights[:, None]), "mem", 0)
    return put_back(analysed, hand_back(winds_all), "mem", 1)


def solution(mesh):
    return jax.shard_map(
        body,
        mesh=mesh,
        in_specs=(
            P("mem", None, "dom", None),
            P(),
            P("dom", "mem", None),
            P("dom", "mem", None),
            P("dom", "mem", None, None),
        ),
        out_specs=P("mem", None, "dom", None),
        check_vma=False,
    )
```

profile of v0, /device:TPU:28, one launch (start us, length us, event | category | flops | bytes accessed | tf_op | source)
XLA Modules:
  0.0 342.6 jit_solution(10296356166149583305)
XLA Ops:
  1.5 4.7 %shard_map.55 = f32[3,3,64,1024]{3,2,1,0:T(8,128)} custom-call(f32[96,128]{1,0:T(8,128)} %broadcast_in_dim.7.coriolis_ref, f32[8,3,64,1024]{3,2,1,0:T(8,128)} %states_ref.2), custom_call_target="tpu_custom_call" | custom-call | flops 47185920 | bytes 4718592 | tf_op jit(solution)/shard_map/pallas_call | solution.py:109
  6.2 2.9 constant_dynamic-slice_fusion.16
  10.5 4.9 %collective-permute-start.1 = (f32[3,3,8,1024]{3,2,1,0:T(8,128)}, f32[3,3,8,1024]{3,2,1,0:T(8,128)}, u32[]{:S(2)}, u32[]{:S(2)}) collective-permute-start(f32[3,3,8,1024]{3,2,1,0:T(8,128)} %get-tuple-element.66), channel_id=1, source_target_pairs={{0,8},{4,12},{8,16},{12,20},{16,24},{28,4},{1,9},{5,13},{9,17},{13... | collective-permute-start | bytes 884744 | tf_op jit(solution)/shard_map/ppermute | solution.py:204
  15.4 3.5 %collective-permute-start.2 = (f32[3,3,8,1024]{3,2,1,0:T(8,128)}, f32[3,3,8,1024]{3,2,1,0:T(8,128)}, u32[]{:S(2)}, u32[]{:S(2)}) collective-permute-start(f32[3,3,8,1024]{3,2,1,0:T(8,128)} %get-tuple-element.67), channel_id=1, source_target_pairs={{0,12},{4,16},{8,20},{12,24},{24,4},{28,8},{1,13},{5,17},{9,21},{1... | collective-permute-start | bytes 884744 | tf_op jit(solution)/shard_map/ppermute | solution.py:204
  21.8 3.1 collective-permute-start.7
  29.5 10.1 %shard_map.56 = (f32[8,64,1024]{2,1,0:T(8,128)}, f32[8,2,64,1024]{3,2,1,0:T(8,128)}) custom-call(f32[2]{0:T(128)} %add_convert_fusion.inside_ref, f32[96,128]{1,0:T(8,128)} %broadcast_in_dim.7.coriolis_ref, f32[8,3,64,1024]{3,2,1,0:T(8,128)} %states_ref.2, f32[8,3,4,1024]{3,2,1,0:T(4,128)} %copy-done.20, f32[8,3,4,1024]{3,2,1,0:T(4,128)} %copy-done.19), custom_call_target="tpu_custom_call" | custom-call | flops 125829120 | bytes 12582912 | tf_op jit(solution)/shard_map/pallas_call | solution.py:127
  42.2 7.4 %collective-permute-start.5 = (f32[3,3,8,1024]{3,2,1,0:T(8,128)S(1)}, f32[3,3,8,1024]{3,2,1,0:T(8,128)}, u32[]{:S(2)}, u32[]{:S(2)}) collective-permute-start(f32[3,3,8,1024]{3,2,1,0:T(8,128)S(1)} %copy-done.31), channel_id=1, source_target_pairs={{0,24},{12,4},{16,8},{20,12},{24,16},{28,20},{1,25},{13,5},{17,9},... | collective-permute-start | bytes 884744 | tf_op jit(solution)/shard_map/ppermute | solution.py:204
  54.7 2.6 collective-permute-start.17
  61.3 4.1 %collective-permute-start.9 = (f32[3,3,8,1024]{3,2,1,0:T(8,128)}, f32[3,3,8,1024]{3,2,1,0:T(8,128)}, u32[]{:S(2)}, u32[]{:S(2)}) collective-permute-start(f32[3,3,8,1024]{3,2,1,0:T(8,128)} %get-tuple-element.76), channel_id=1, source_target_pairs={{24,28},{28,0},{25,29},{29,1},{26,30},{30,2},{27,31},{31,3}} | collective-permute-start | bytes 884744 | tf_op jit(solution)/shard_map/ppermute | solution.py:204
  67.3 15.9 %collective-permute-start.20 = (f32[5,8,1024]{2,1,0:T(8,128)}, f32[5,8,1024]{2,1,0:T(8,128)S(1)}, u32[]{:S(2)}, u32[]{:S(2)}) collective-permute-start(f32[5,8,1024]{2,1,0:T(8,128)} %get-tuple-element.88), channel_id=1, source_target_pairs={{0,20},{4,24},{8,28},{12,0},{16,4},{20,8},{24,12},{28,16},{1,21},{... | collective-permute-start | bytes 491528 | tf_op jit(solution)/shard_map/ppermute | solution.py:204
  83.2 3.6 %collective-permute-start.22 = (f32[5,8,1024]{2,1,0:T(8,128)}, f32[5,8,1024]{2,1,0:T(8,128)S(1)}, u32[]{:S(2)}, u32[]{:S(2)}) collective-permute-start(f32[5,8,1024]{2,1,0:T(8,128)} %get-tuple-element.90), channel_id=1, source_target_pairs={{0,28},{4,0},{8,4},{12,8},{16,12},{20,16},{24,20},{28,24},{1,29},{... | collective-permute-start | bytes 491528 | tf_op jit(solution)/shard_map/ppermute | solution.py:204
  89.4 2.4 collective-permute-done.21
  93.1 4.7 %collective-permute-done.22 = f32[5,8,1024]{2,1,0:T(8,128)S(1)} collective-permute-done((f32[5,8,1024]{2,1,0:T(8,128)}, f32[5,8,1024]{2,1,0:T(8,128)S(1)}, u32[]{:S(2)}, u32[]{:S(2)}) %collective-permute-start.22) | collective-permute-done | bytes 163872 | tf_op jit(solution)/shard_map/ppermute | solution.py:204
  105.3 11.4 %collective-permute-done.11 = f32[3,3,8,1024]{3,2,1,0:T(8,128)S(1)} collective-permute-done((f32[3,3,8,1024]{3,2,1,0:T(8,128)}, f32[3,3,8,1024]{3,2,1,0:T(8,128)S(1)}, u32[]{:S(2)}, u32[]{:S(2)}) %collective-permute-start.11) | collective-permute-done | bytes 294944 | tf_op jit(solution)/shard_map/ppermute | solution.py:204
  117.9 3.2 collective-permute-start.33
  138.4 6.8 %fusion.18 = f32[8,64,512]{2,1,0:T(8,128)S(1)} fusion(s32[8,512]{1,0:T(8,128)S(1)} %bitcast.113, f32[64,8,1024]{2,1,0:T(8,128)S(1)} %constant_dynamic-update-slice_fusion, f32[8,512]{1,0:T(8,128)S(1)} %bitcast.115), kind=kOutput, calls=%fused_computation.35 | convolution fusion | flops 3225944064 | bytes 3178496 | tf_op jit(solution)/shard_map/erl,rlo->reo/dot_general | solution.py:164
  148.4 18.8 %concatenate.64 = f32[64,1,8,8,128]{4,0,3,2,1:T(8,128)S(1)} concatenate(f32[3,1,8,8,128]{4,0,3,2,1:T(4,128)} %copy.23, f32[3,1,8,8,128]{4,0,3,2,1:T(4,128)} %copy.24, f32[3,1,8,8,128]{4,0,3,2,1:T(4,128)} %copy.25, f32[3,1,8,8,128]{4,0,3,2,1:T(4,128)} %copy.26, f32[3,1,8,8,128]{4,0,3,2,1:T(4,128)} %copy.27, f32[3,1,8,8,128]{4,0,3,2,1:T(4,128)} %copy.28, ...), dimensions={0} | concatenate | bytes 4194304 | tf_op jit(solution)/shard_map/concatenate | solution.py:277
  167.3 8.3 %fusion.12 = f32[64,1,8,8,128]{4,0,3,2,1:T(8,128)S(1)} fusion(f32[64,1,8,8,128]{4,0,3,2,1:T(8,128)S(1)} %concatenate.64, s32[8,8,64]{2,1,0:T(8,128)} %get-tuple-element.174, s32[8,8,64]{2,1,0:T(8,128)} %get-tuple-element.175, s32[8,8,64]{2,1,0:T(8,128)} %get-tuple-element.173, f32[8,8,64]{2,1,0:T(8,128)} %divide_multiply_fusion), kind=kOutput, calls=%fused_computation.31 | convolution fusion | flops 405274624 | bytes 4259840 | tf_op jit(solution)/shard_map/rbek,kfrbc->efrbc/dot_general | solution.py:192
  176.6 3.5 %broadcast_in_dim.6 = f32[8,3,64,1024]{3,2,1,0:T(8,128)} broadcast(f32[]{:T(128)} %constant.112.clone.1), dimensions={} | broadcast | bytes 6291460 | tf_op jit(solution)/shard_map/broadcast_in_dim | solution.py:291
  191.1 3.7 %collective-permute-start.23 = (f32[8,1,8,1024]{3,1,2,0:T(1,128)}, f32[8,1,8,1024]{3,1,2,0:T(1,128)S(1)}, u32[]{:S(2)}, u32[]{:S(2)}) collective-permute-start(f32[8,1,8,1024]{3,1,2,0:T(1,128)} %bitcast.37), channel_id=1, source_target_pairs={{0,4},{4,8},{8,12},{12,16},{16,20},{20,24},{24,28},{28,0},{1,5},{5... | collective-permute-start | bytes 786440 | tf_op jit(solution)/shard_map/ppermute | solution.py:204
  199.4 2.4 collective-permute-start.26
  201.8 5.3 %collective-permute-done.36 = f32[5,2,8,1024]{3,2,1,0:T(8,128)S(1)} collective-permute-done((f32[5,2,8,1024]{3,2,1,0:T(8,128)S(1)}, f32[5,2,8,1024]{3,2,1,0:T(8,128)S(1)}, u32[]{:S(2)}, u32[]{:S(2)}) %collective-permute-start.36) | collective-permute-done | bytes 327712 | tf_op jit(solution)/shard_map/ppermute | solution.py:204
  207.1 17.4 %collective-permute-start.27 = (f32[8,1,8,1024]{3,1,2,0:T(1,128)}, f32[8,1,8,1024]{3,1,2,0:T(1,128)}, u32[]{:S(2)}, u32[]{:S(2)}) collective-permute-start(f32[8,1,8,1024]{3,1,2,0:T(1,128)} %bitcast.41), channel_id=1, source_target_pairs={{0,20},{4,24},{8,28},{12,0},{16,4},{20,8},{24,12},{28,16},{1,21},{... | collective-permute-start | bytes 786440 | tf_op jit(solution)/shard_map/ppermute | solution.py:204
  224.6 9.1 %fusion.5 = f32[64,2,8,8,128]{4,0,1,3,2:T(8,128)S(1)} fusion(f32[64,2,8,8,128]{4,2,3,1,0:T(8,128)S(1)} %bitcast.114, s32[8,8,64]{2,1,0:T(8,128)S(1)} %copy-done.35, s32[8,8,64]{2,1,0:T(8,128)S(1)} %copy-done.36, s32[8,8,64]{2,1,0:T(8,128)S(1)} %copy-done.34, f32[8,8,64]{2,1,0:T(8,128)S(1)} %copy-done.33), kind=kOutput, calls=%fused_computation.22 | convolution fusion | flops 807927808 | bytes 8454144 | tf_op jit(solution)/shard_map/rbek,kfrbc->efrbc/dot_general | solution.py:192
  238.0 2.0 copy.66
  248.6 3.4 collective-permute-start.29
  253.7 3.2 collective-permute-start.37
  262.7 9.2 %collective-permute-start.40 = (f32[8,2,8,1024]{3,2,1,0:T(8,128)S(1)}, f32[8,2,8,1024]{3,2,1,0:T(8,128)S(1)}, u32[]{:S(2)}, u32[]{:S(2)}) collective-permute-start(f32[8,2,8,1024]{3,2,1,0:T(8,128)S(1)} %copy-done.18), channel_id=1, source_target_pairs={{0,16},{4,20},{8,24},{12,28},{16,0},{20,4},{24,8},{28,12},{1,17},{... | collective-permute-start | bytes 1572872 | tf_op jit(solution)/shard_map/ppermute | solution.py:204
  272.7 12.3 %collective-permute-start.41 = (f32[8,2,8,1024]{3,2,1,0:T(8,128)S(1)}, f32[8,2,8,1024]{3,2,1,0:T(8,128)S(1)}, u32[]{:S(2)}, u32[]{:S(2)}) collective-permute-start(f32[8,2,8,1024]{3,2,1,0:T(8,128)S(1)} %copy-done.17), channel_id=1, source_target_pairs={{0,20},{4,24},{8,28},{12,0},{16,4},{20,8},{24,12},{28,16},{1,21},{... | collective-permute-start | bytes 1572872 | tf_op jit(solution)/shard_map/ppermute | solution.py:204
  287.4 3.8 %collective-permute-start.43 = (f32[8,2,8,1024]{3,2,1,0:T(8,128)S(1)}, f32[8,2,8,1024]{3,2,1,0:T(8,128)S(1)}, u32[]{:S(2)}, u32[]{:S(2)}) collective-permute-start(f32[8,2,8,1024]{3,2,1,0:T(8,128)S(1)} %copy-done.15), channel_id=1, source_target_pairs={{0,28},{4,0},{8,4},{12,8},{16,12},{20,16},{24,20},{28,24},{1,29},{... | collective-permute-start | bytes 1572872 | tf_op jit(solution)/shard_map/ppermute | solution.py:204
  292.9 38.9 %collective-permute-done.40 = f32[8,2,8,1024]{3,2,1,0:T(8,128)S(1)} collective-permute-done((f32[8,2,8,1024]{3,2,1,0:T(8,128)S(1)}, f32[8,2,8,1024]{3,2,1,0:T(8,128)S(1)}, u32[]{:S(2)}, u32[]{:S(2)}) %collective-permute-start.40) | collective-permute-done | bytes 524320 | tf_op jit(solution)/shard_map/ppermute | solution.py:204
  332.6 7.5 %collective-permute-done.41 = f32[8,2,8,1024]{3,2,1,0:T(8,128)S(1)} collective-permute-done((f32[8,2,8,1024]{3,2,1,0:T(8,128)S(1)}, f32[8,2,8,1024]{3,2,1,0:T(8,128)S(1)}, u32[]{:S(2)}, u32[]{:S(2)}) %collective-permute-start.41) | collective-permute-done | bytes 524320 | tf_op jit(solution)/shard_map/ppermute | solution.py:204
  (268 shorter events, 101.3 us)
Async XLA Ops:
  9.1 33.1 %collective-permute-start = (f32[3,3,8,1024]{3,2,1,0:T(8,128)}, f32[3,3,8,1024]{3,2,1,0:T(8,128)}, u32[]{:S(2)}, u32[]{:S(2)}) collective-permute-start(f32[3,3,8,1024]{3,2,1,0:T(8,128)} %get-tuple-element.65), channel_id=1, source_target_pairs={{0,4},{4,8},{8,12},{12,16},{16,20},{20,24},{1,5},{5,9},{9,13},{13,... | collective-permute-start | bytes 884744 | tf_op jit(solution)/shard_map/ppermute | solution.py:204
  10.5 39.2 %collective-permute-start.1 = (f32[3,3,8,1024]{3,2,1,0:T(8,128)}, f32[3,3,8,1024]{3,2,1,0:T(8,128)}, u32[]{:S(2)}, u32[]{:S(2)}) collective-permute-start(f32[3,3,8,1024]{3,2,1,0:T(8,128)} %get-tuple-element.66), channel_id=1, source_target_pairs={{0,8},{4,12},{8,16},{12,20},{16,24},{28,4},{1,9},{5,13},{9,17},{13... | collective-permute-start | bytes 884744 | tf_op jit(solution)/shard_map/ppermute | solution.py:204
  15.4 38.2 %collective-permute-start.2 = (f32[3,3,8,1024]{3,2,1,0:T(8,128)}, f32[3,3,8,1024]{3,2,1,0:T(8,128)}, u32[]{:S(2)}, u32[]{:S(2)}) collective-permute-start(f32[3,3,8,1024]{3,2,1,0:T(8,128)} %get-tuple-element.67), channel_id=1, source_target_pairs={{0,12},{4,16},{8,20},{12,24},{24,4},{28,8},{1,13},{5,17},{9,21},{1... | collective-permute-start | bytes 884744 | tf_op jit(solution)/shard_map/ppermute | solution.py:204
  26.8 27.9 %collective-permute-start.3 = (f32[3,3,8,1024]{3,2,1,0:T(8,128)}, f32[3,3,8,1024]{3,2,1,0:T(8,128)S(1)}, u32[]{:S(2)}, u32[]{:S(2)}) collective-permute-start(f32[3,3,8,1024]{3,2,1,0:T(8,128)} %get-tuple-element.68), channel_id=1, source_target_pairs={{0,16},{4,20},{8,24},{20,4},{24,8},{28,12},{1,17},{5,21},{9,25},{2... | collective-permute-start | bytes 884744 | tf_op jit(solution)/shard_map/ppermute | solution.py:204
  28.1 29.2 %collective-permute-start.4 = (f32[3,3,8,1024]{3,2,1,0:T(8,128)}, f32[3,3,8,1024]{3,2,1,0:T(8,128)S(1)}, u32[]{:S(2)}, u32[]{:S(2)}) collective-permute-start(f32[3,3,8,1024]{3,2,1,0:T(8,128)} %get-tuple-element.69), channel_id=1, source_target_pairs={{0,20},{4,24},{16,4},{20,8},{24,12},{28,16},{1,21},{5,25},{17,5},{... | collective-permute-start | bytes 884744 | tf_op jit(solution)/shard_map/ppermute | solution.py:204
  57.3 25.9 %collective-permute-start.18 = (f32[5,8,1024]{2,1,0:T(8,128)}, f32[5,8,1024]{2,1,0:T(8,128)S(1)}, u32[]{:S(2)}, u32[]{:S(2)}) collective-permute-start(f32[5,8,1024]{2,1,0:T(8,128)} %get-tuple-element.86), channel_id=1, source_target_pairs={{0,12},{4,16},{8,20},{12,24},{16,28},{20,0},{24,4},{28,8},{1,13},{... | collective-permute-start | bytes 491528 | tf_op jit(solution)/shard_map/ppermute | solution.py:204
  58.5 24.7 %collective-permute-start.19 = (f32[5,8,1024]{2,1,0:T(8,128)}, f32[5,8,1024]{2,1,0:T(8,128)S(1)}, u32[]{:S(2)}, u32[]{:S(2)}) collective-permute-start(f32[5,8,1024]{2,1,0:T(8,128)} %get-tuple-element.87), channel_id=1, source_target_pairs={{0,16},{4,20},{8,24},{12,28},{16,0},{20,4},{24,8},{28,12},{1,17},{... | collective-permute-start | bytes 491528 | tf_op jit(solution)/shard_map/ppermute | solution.py:204
  61.3 37.8 %collective-permute-start.9 = (f32[3,3,8,1024]{3,2,1,0:T(8,128)}, f32[3,3,8,1024]{3,2,1,0:T(8,128)}, u32[]{:S(2)}, u32[]{:S(2)}) collective-permute-start(f32[3,3,8,1024]{3,2,1,0:T(8,128)} %get-tuple-element.76), channel_id=1, source_target_pairs={{24,28},{28,0},{25,29},{29,1},{26,30},{30,2},{27,31},{31,3}} | collective-permute-start | bytes 884744 | tf_op jit(solution)/shard_map/ppermute | solution.py:204
  65.4 35.0 %collective-permute-start.10 = (f32[3,3,8,1024]{3,2,1,0:T(8,128)}, f32[3,3,8,1024]{3,2,1,0:T(8,128)}, u32[]{:S(2)}, u32[]{:S(2)}) collective-permute-start(f32[3,3,8,1024]{3,2,1,0:T(8,128)} %get-tuple-element.77), channel_id=1, source_target_pairs={{20,28},{24,0},{21,29},{25,1},{22,30},{26,2},{23,31},{27,3}} | collective-permute-start | bytes 884744 | tf_op jit(solution)/shard_map/ppermute | solution.py:204
  67.3 20.8 %collective-permute-start.20 = (f32[5,8,1024]{2,1,0:T(8,128)}, f32[5,8,1024]{2,1,0:T(8,128)S(1)}, u32[]{:S(2)}, u32[]{:S(2)}) collective-permute-start(f32[5,8,1024]{2,1,0:T(8,128)} %get-tuple-element.88), channel_id=1, source_target_pairs={{0,20},{4,24},{8,28},{12,0},{16,4},{20,8},{24,12},{28,16},{1,21},{... | collective-permute-start | bytes 491528 | tf_op jit(solution)/shard_map/ppermute | solution.py:204
  88.1 28.6 %collective-permute-start.11 = (f32[3,3,8,1024]{3,2,1,0:T(8,128)}, f32[3,3,8,1024]{3,2,1,0:T(8,128)S(1)}, u32[]{:S(2)}, u32[]{:S(2)}) collective-permute-start(f32[3,3,8,1024]{3,2,1,0:T(8,128)} %get-tuple-element.78), channel_id=1, source_target_pairs={{16,28},{20,0},{17,29},{21,1},{18,30},{22,2},{19,31},{23,3}} | collective-permute-start | bytes 884744 | tf_op jit(solution)/shard_map/ppermute | solution.py:204
  91.8 24.9 %collective-permute-start.12 = (f32[3,3,8,1024]{3,2,1,0:T(8,128)}, f32[3,3,8,1024]{3,2,1,0:T(8,128)S(1)}, u32[]{:S(2)}, u32[]{:S(2)}) collective-permute-start(f32[3,3,8,1024]{3,2,1,0:T(8,128)} %get-tuple-element.79), channel_id=1, source_target_pairs={{12,28},{16,0},{13,29},{17,1},{14,30},{18,2},{15,31},{19,3}} | collective-permute-start | bytes 884744 | tf_op jit(solution)/shard_map/ppermute | solution.py:204
  97.8 18.9 %collective-permute-start.13 = (f32[3,3,8,1024]{3,2,1,0:T(8,128)}, f32[3,3,8,1024]{3,2,1,0:T(8,128)}, u32[]{:S(2)}, u32[]{:S(2)}) collective-permute-start(f32[3,3,8,1024]{3,2,1,0:T(8,128)} %get-tuple-element.80), channel_id=1, source_target_pairs={{8,28},{12,0},{9,29},{13,1},{10,30},{14,2},{11,31},{15,3}} | collective-permute-start | bytes 884744 | tf_op jit(solution)/shard_map/ppermute | solution.py:204
  100.4 20.7 %collective-permute-start.15 = (f32[3,3,8,1024]{3,2,1,0:T(8,128)S(1)}, f32[3,3,8,1024]{3,2,1,0:T(8,128)}, u32[]{:S(2)}, u32[]{:S(2)}) collective-permute-start(f32[3,3,8,1024]{3,2,1,0:T(8,128)S(1)} %get-tuple-element.82), channel_id=1, source_target_pairs={{0,28},{4,0},{1,29},{5,1},{2,30},{6,2},{3,31},{7,3}} | collective-permute-start | bytes 884744 | tf_op jit(solution)/shard_map/ppermute | solution.py:204
  116.7 69.5 %collective-permute-start.30 = (f32[5,2,8,1024]{3,2,1,0:T(8,128)}, f32[5,2,8,1024]{3,2,1,0:T(8,128)}, u32[]{:S(2)}, u32[]{:S(2)}) collective-permute-start(f32[5,2,8,1024]{3,2,1,0:T(8,128)} %get-tuple-element.116), channel_id=1, source_target_pairs={{0,4},{4,8},{8,12},{12,16},{16,20},{20,24},{24,28},{28,0},{1,5},{5... | collective-permute-start | bytes 983048 | tf_op jit(solution)/shard_map/ppermute | solution.py:204
  116.7 72.2 %collective-permute-start.31 = (f32[5,2,8,1024]{3,2,1,0:T(8,128)}, f32[5,2,8,1024]{3,2,1,0:T(8,128)}, u32[]{:S(2)}, u32[]{:S(2)}) collective-permute-start(f32[5,2,8,1024]{3,2,1,0:T(8,128)} %get-tuple-element.117), channel_id=1, source_target_pairs={{0,8},{4,12},{8,16},{12,20},{16,24},{20,28},{24,0},{28,4},{1,9},{5... | collective-permute-start | bytes 983048 | tf_op jit(solution)/shard_map/ppermute | solution.py:204
  116.8 74.3 %collective-permute-start.32 = (f32[5,2,8,1024]{3,2,1,0:T(8,128)}, f32[5,2,8,1024]{3,2,1,0:T(8,128)}, u32[]{:S(2)}, u32[]{:S(2)}) collective-permute-start(f32[5,2,8,1024]{3,2,1,0:T(8,128)} %get-tuple-element.118), channel_id=1, source_target_pairs={{0,12},{4,16},{8,20},{12,24},{16,28},{20,0},{24,4},{28,8},{1,13},{... | collective-permute-start | bytes 983048 | tf_op jit(solution)/shard_map/ppermute | solution.py:204
  117.9 77.8 %collective-permute-start.33 = (f32[5,2,8,1024]{3,2,1,0:T(8,128)}, f32[5,2,8,1024]{3,2,1,0:T(8,128)}, u32[]{:S(2)}, u32[]{:S(2)}) collective-permute-start(f32[5,2,8,1024]{3,2,1,0:T(8,128)} %get-tuple-element.119), channel_id=1, source_target_pairs={{0,16},{4,20},{8,24},{12,28},{16,0},{20,4},{24,8},{28,12},{1,17},{... | collective-permute-start | bytes 983048 | tf_op jit(solution)/shard_map/ppermute | solution.py:204
  121.2 76.6 %collective-permute-start.34 = (f32[5,2,8,1024]{3,2,1,0:T(8,128)}, f32[5,2,8,1024]{3,2,1,0:T(8,128)}, u32[]{:S(2)}, u32[]{:S(2)}) collective-permute-start(f32[5,2,8,1024]{3,2,1,0:T(8,128)} %get-tuple-element.120), channel_id=1, source_target_pairs={{0,20},{4,24},{8,28},{12,0},{16,4},{20,8},{24,12},{28,16},{1,21},{... | collective-permute-start | bytes 983048 | tf_op jit(solution)/shard_map/ppermute | solution.py:204
  191.1 56.7 %collective-permute-start.23 = (f32[8,1,8,1024]{3,1,2,0:T(1,128)}, f32[8,1,8,1024]{3,1,2,0:T(1,128)S(1)}, u32[]{:S(2)}, u32[]{:S(2)}) collective-permute-start(f32[8,1,8,1024]{3,1,2,0:T(1,128)} %bitcast.37), channel_id=1, source_target_pairs={{0,4},{4,8},{8,12},{12,16},{16,20},{20,24},{24,28},{28,0},{1,5},{5... | collective-permute-start | bytes 786440 | tf_op jit(solution)/shard_map/ppermute | solution.py:204
  195.7 52.9 %collective-permute-start.24 = (f32[8,1,8,1024]{3,1,2,0:T(1,128)}, f32[8,1,8,1024]{3,1,2,0:T(1,128)}, u32[]{:S(2)}, u32[]{:S(2)}) collective-permute-start(f32[8,1,8,1024]{3,1,2,0:T(1,128)} %bitcast.38), channel_id=1, source_target_pairs={{0,8},{4,12},{8,16},{12,20},{16,24},{20,28},{24,0},{28,4},{1,9},{5... | collective-permute-start | bytes 786440 | tf_op jit(solution)/shard_map/ppermute | solution.py:204
  197.7 56.0 %collective-permute-start.25 = (f32[8,1,8,1024]{3,1,2,0:T(1,128)}, f32[8,1,8,1024]{3,1,2,0:T(1,128)}, u32[]{:S(2)}, u32[]{:S(2)}) collective-permute-start(f32[8,1,8,1024]{3,1,2,0:T(1,128)} %bitcast.39), channel_id=1, source_target_pairs={{0,12},{4,16},{8,20},{12,24},{16,28},{20,0},{24,4},{28,8},{1,13},{... | collective-permute-start | bytes 786440 | tf_op jit(solution)/shard_map/ppermute | solution.py:204
  199.4 59.3 %collective-permute-start.26 = (f32[8,1,8,1024]{3,1,2,0:T(1,128)}, f32[8,1,8,1024]{3,1,2,0:T(1,128)}, u32[]{:S(2)}, u32[]{:S(2)}) collective-permute-start(f32[8,1,8,1024]{3,1,2,0:T(1,128)} %bitcast.40), channel_id=1, source_target_pairs={{0,16},{4,20},{8,24},{12,28},{16,0},{20,4},{24,8},{28,12},{1,17},{... | collective-permute-start | bytes 786440 | tf_op jit(solution)/shard_map/ppermute | solution.py:204
  207.1 53.9 %collective-permute-start.27 = (f32[8,1,8,1024]{3,1,2,0:T(1,128)}, f32[8,1,8,1024]{3,1,2,0:T(1,128)}, u32[]{:S(2)}, u32[]{:S(2)}) collective-permute-start(f32[8,1,8,1024]{3,1,2,0:T(1,128)} %bitcast.41), channel_id=1, source_target_pairs={{0,20},{4,24},{8,28},{12,0},{16,4},{20,8},{24,12},{28,16},{1,21},{... | collective-permute-start | bytes 786440 | tf_op jit(solution)/shard_map/ppermute | solution.py:204
  248.6 24.0 %collective-permute-start.29 = (f32[8,1,8,1024]{3,1,2,0:T(1,128)}, f32[8,1,8,1024]{3,1,2,0:T(1,128)S(1)}, u32[]{:S(2)}, u32[]{:S(2)}) collective-permute-start(f32[8,1,8,1024]{3,1,2,0:T(1,128)} %bitcast.111), channel_id=1, source_target_pairs={{0,28},{4,0},{8,4},{12,8},{16,12},{20,16},{24,20},{28,24},{1,29},{... | collective-permute-start | bytes 786440 | tf_op jit(solution)/shard_map/ppermute | solution.py:204
  253.7 32.8 %collective-permute-start.37 = (f32[8,2,8,1024]{3,2,1,0:T(8,128)}, f32[8,2,8,1024]{3,2,1,0:T(8,128)S(1)}, u32[]{:S(2)}, u32[]{:S(2)}) collective-permute-start(f32[8,2,8,1024]{3,2,1,0:T(8,128)} %slice.215), channel_id=1, source_target_pairs={{0,4},{4,8},{8,12},{12,16},{16,20},{20,24},{24,28},{28,0},{1,5},{5... | collective-permute-start | bytes 1572872 | tf_op jit(solution)/shard_map/ppermute | solution.py:204
  258.7 28.7 %collective-permute-start.38 = (f32[8,2,8,1024]{3,2,1,0:T(8,128)S(1)}, f32[8,2,8,1024]{3,2,1,0:T(8,128)S(1)}, u32[]{:S(2)}, u32[]{:S(2)}) collective-permute-start(f32[8,2,8,1024]{3,2,1,0:T(8,128)S(1)} %slice.217), channel_id=1, source_target_pairs={{0,8},{4,12},{8,16},{12,20},{16,24},{20,28},{24,0},{28,4},{1,9},{5... | collective-permute-start | bytes 1572872 | tf_op jit(solution)/shard_map/ppermute | solution.py:204
  261.0 31.0 %collective-permute-start.39 = (f32[8,2,8,1024]{3,2,1,0:T(8,128)S(1)}, f32[8,2,8,1024]{3,2,1,0:T(8,128)S(1)}, u32[]{:S(2)}, u32[]{:S(2)}) collective-permute-start(f32[8,2,8,1024]{3,2,1,0:T(8,128)S(1)} %slice.219), channel_id=1, source_target_pairs={{0,12},{4,16},{8,20},{12,24},{16,28},{20,0},{24,4},{28,8},{1,13},{... | collective-permute-start | bytes 1572872 | tf_op jit(solution)/shard_map/ppermute | solution.py:204
  262.7 69.1 %collective-permute-start.40 = (f32[8,2,8,1024]{3,2,1,0:T(8,128)S(1)}, f32[8,2,8,1024]{3,2,1,0:T(8,128)S(1)}, u32[]{:S(2)}, u32[]{:S(2)}) collective-permute-start(f32[8,2,8,1024]{3,2,1,0:T(8,128)S(1)} %copy-done.18), channel_id=1, source_target_pairs={{0,16},{4,20},{8,24},{12,28},{16,0},{20,4},{24,8},{28,12},{1,17},{... | collective-permute-start | bytes 1572872 | tf_op jit(solution)/shard_map/ppermute | solution.py:204
  272.7 67.4 %collective-permute-start.41 = (f32[8,2,8,1024]{3,2,1,0:T(8,128)S(1)}, f32[8,2,8,1024]{3,2,1,0:T(8,128)S(1)}, u32[]{:S(2)}, u32[]{:S(2)}) collective-permute-start(f32[8,2,8,1024]{3,2,1,0:T(8,128)S(1)} %copy-done.17), channel_id=1, source_target_pairs={{0,20},{4,24},{8,28},{12,0},{16,4},{20,8},{24,12},{28,16},{1,21},{... | collective-permute-start | bytes 1572872 | tf_op jit(solution)/shard_map/ppermute | solution.py:204
  286.6 54.3 %collective-permute-start.42 = (f32[8,2,8,1024]{3,2,1,0:T(8,128)S(1)}, f32[8,2,8,1024]{3,2,1,0:T(8,128)S(1)}, u32[]{:S(2)}, u32[]{:S(2)}) collective-permute-start(f32[8,2,8,1024]{3,2,1,0:T(8,128)S(1)} %copy-done.16), channel_id=1, source_target_pairs={{0,24},{4,28},{8,0},{12,4},{16,8},{20,12},{24,16},{28,20},{1,25},{... | collective-permute-start | bytes 1572872 | tf_op jit(solution)/shard_map/ppermute | solution.py:204
  287.4 54.3 %collective-permute-start.43 = (f32[8,2,8,1024]{3,2,1,0:T(8,128)S(1)}, f32[8,2,8,1024]{3,2,1,0:T(8,128)S(1)}, u32[]{:S(2)}, u32[]{:S(2)}) collective-permute-start(f32[8,2,8,1024]{3,2,1,0:T(8,128)S(1)} %copy-done.15), channel_id=1, source_target_pairs={{0,28},{4,0},{8,4},{12,8},{16,12},{20,16},{24,20},{28,24},{1,29},{... | collective-permute-start | bytes 1572872 | tf_op jit(solution)/shard_map/ppermute | solution.py:204
  (52 other events, 816.9 us)
where the time goes:
time: 345 us; the launch traced here: 343 us
  starting transfers between devices  127 us (37%)
  local copies, waits for them, and re-layouts  92.5 us (27%)
  waiting for transfers between devices  71.1 us (21%)
  matrix products  25.2 us (7%)
  Pallas kernels  14.8 us (4%)
  other arithmetic  10.4 us (3%)
    ppermute x42, starting transfers between devices, send_all(): lax.ppermute(pieces[d], axis, shifts(count, d, targets))  123 us
    ppermute x42, waiting for transfers between devices, send_all(): lax.ppermute(pieces[d], axis, shifts(count, d, targets))  71.1 us
    concatenate x26, local copies, waits for them, and re-layouts, body(): heights = jnp.concatenate([a[:, 0] for a in firsts] + late_heights, axis=0)  30.5 us
    slice x26, local copies, waits for them, and re-layouts, hand_back(): updated[d * members_dev:(d + 1) * members_dev]  19.6 us
    dot_general x2, matrix products, merge_fields(): jnp.einsum('rbek,kfrbc->efrbc', mixing, blocks, precision=lax.Precision.H...  17.4 us
    dynamic_update_slice x16, local copies, waits for them, and re-layouts, put_back(): whole = lax.dynamic_update_slice(whole, piece, (0, field, start, 0))  16.5 us
    pallas_call x1, Pallas kernels, forecast(): pl.pallas_call(functools.partial(forecast_steps, margin), grid=(members,)...  10.1 us
  transfers between devices with their start and end apart: 44, of which 7 were waited for; matrix products, arithmetic and copies ran while one was open for 36% of the time, Pallas kernels for 3%

commit v1 on v0

--- a/solution.py
+++ b/solution.py
@@ -13,7 +13,6 @@
 STEPS = 2
 SUBLANES = 8
 LANES = 128
-EARLY_MEMBERS = 3
 
 
 FLOW_FACTOR = 1.0
@@ -34,9 +33,8 @@
     return before, after
 
 
-def early_kernel(margin, coriolis_ref, states_ref, all_ref, here, there):
-    forecast_steps(margin, None, coriolis_ref, states_ref, None, None,
-                   all_ref.at[:, 0], all_ref.at[:, 1:], here, there)
+def early_kernel(margin, coriolis_ref, states_ref, height_ref, here, there):
+    forecast_steps(margin, None, coriolis_ref, states_ref, None, None, height_ref, None, here, there)
 
 
 def forecast_steps(margin, inside_ref, coriolis_ref, states_ref, before_ref, after_ref,
@@ -75,6 +73,8 @@
             new[0, tile(t), :] = height
             if final and 1 < t < last:
                 height_ref[0, tile(t - 2), :] = height
+        if final and winds_ref is None:
+            break
         for t in range(1, last + 1) if with_halo and not final else range(2, last):
             factor = jnp.concatenate([coriolis_ref[tile(t), :]] * (width // LANES), axis=1)
             east_old, north_old = old[1, tile(t), :], old[2, tile(t), :]
@@ -99,24 +99,25 @@
     return jnp.broadcast_to(factors[:, None], (frame, LANES))
 
 
-def forecast_cost(members, states):
-    size = members * states.size // states.shape[0]
-    return pl.CostEstimate(flops=40 * size * STEPS, bytes_accessed=8 * size, transcendentals=0)
-
-
-def early_forecast(states, factors, early):
-    fields, rows, width = states.shape[1:]
+def forecast_cost(states):
+    return pl.CostEstimate(
+        flops=40 * states.size * STEPS, bytes_accessed=8 * states.size, transcendentals=0
+    )
+
+
+def early_heights(states, factors):
+    members, fields, rows, width = states.shape
     return pl.pallas_call(
         functools.partial(early_kernel, 2 * STEPS),
-        grid=(early,),
+        grid=(members,),
         in_specs=[
             pl.BlockSpec(factors.shape, lambda m: (0, 0)),
             pl.BlockSpec((1, fields, rows, width), lambda m: (m, 0, 0, 0)),
         ],
-        out_specs=pl.BlockSpec((1, fields, rows, width), lambda m: (m, 0, 0, 0)),
-        out_shape=jax.ShapeDtypeStruct((early, fields, rows, width), jnp.float32),
+        out_specs=pl.BlockSpec((1, rows, width), lambda m: (m, 0, 0)),
+        out_shape=jax.ShapeDtypeStruct((members, rows, width), jnp.float32),
         scratch_shapes=[pltpu.VMEM((fields, factors.shape[0], width), jnp.float32)] * 2,
-        cost_estimate=forecast_cost(early, states),
+        cost_estimate=forecast_cost(states),
     )(factors, states)
 
 
@@ -143,7 +144,7 @@
             jax.ShapeDtypeStruct((members, fields - 1, rows, width), jnp.float32),
         ],
         scratch_shapes=[pltpu.VMEM((fields, factors.shape[0], width), jnp.float32)] * 2,
-        cost_estimate=forecast_cost(members, states),
+        cost_estimate=forecast_cost(states),
     )(inside, factors, states, before, after)
 
 
@@ -226,17 +227,11 @@
     return whole
 
 
-def relative_draws(draws, axis, members_dev, early):
+def relative_draws(draws, axis, members_dev):
     count = lax.axis_size(axis)
     own = lax.axis_index(axis)
-    member = draws % members_dev
     distance = lax.rem(own + count - draws // members_dev, count)
-    late = members_dev - early
-    place = jnp.where(
-        member < early,
-        distance * early + member,
-        count * early + distance * late + member - early,
-    )
+    place = distance * members_dev + draws % members_dev
     split = place.reshape(place.shape[:-1] + (3, count, members_dev))
     doubled = jnp.concatenate([split, split], axis=-2)
     turned = lax.dynamic_slice_in_dim(doubled, own, count, axis=-2)
@@ -249,7 +244,6 @@
     own = lax.axis_index("mem")
     band_index = lax.axis_index("dom")
     margin = 2 * STEPS
-    early = EARLY_MEMBERS
     piece = count_of_rows // count
     inner = [
         j for j in range(count)
@@ -258,28 +252,23 @@
     outer = [j for j in range(count) if j not in inner]
     factors = coriolis_frame(coriolis, band_index, count_of_rows)
 
-    first = early_forecast(particle_states, factors, early)
-    first_pieces = row_pieces(first, "mem", 2)
-    first_inner = send_all(first_pieces, "mem", inner)
-    states, _ = lax.optimization_barrier((particle_states, first_pieces))
+    first = row_pieces(early_heights(particle_states, factors), "mem", 1)
+    inner_heights = send_all(first, "mem", inner)
+    states, _ = lax.optimization_barrier((particle_states, first))
     before, after = edge_rows(states, "dom", 2, margin)
     height, winds = forecast(states, before, after, factors, band_index, lax.axis_size("dom"))
-    again = jnp.concatenate([height[:early, None], winds[:early]], axis=1)
-    first_outer = send_all(row_pieces(again, "mem", 2), "mem", outer)
-    late_heights = send_all(row_pieces(height[early:], "mem", 1), "mem")
-    late_winds = send_all(row_pieces(winds[early:], "mem", 2), "mem")
-    first_inner, first_outer, late_heights = lax.optimization_barrier(
-        (first_inner, first_outer, late_heights)
-    )
-
+    outer_heights = send_all(row_pieces(height, "mem", 1), "mem", outer)
+    winds_all = send_all(row_pieces(winds, "mem", 2), "mem")
+    inner_heights, outer_heights = lax.optimization_barrier((inner_heights, outer_heights))
     is_outer = jnp.any(jnp.stack([own == j for j in outer]))
-    firsts = [jnp.where(is_outer, a, b) for a, b in zip(first_outer, first_inner)]
-    heights = jnp.concatenate([a[:, 0] for a in firsts] + late_heights, axis=0)
-    winds_all = jnp.concatenate([a[:, 1:] for a in firsts] + late_winds, axis=0)
+    heights = jnp.concatenate(
+        [jnp.where(is_outer, a, b) for a, b in zip(outer_heights, inner_heights)], axis=0
+    )
+    winds_all = jnp.concatenate(winds_all, axis=0)
 
     cells = observed_cells[0]
     values = observed_values[0]
-    draws = relative_draws(resample_draws[0], "mem", members_dev, early)
+    draws = relative_draws(resample_draws[0], "mem", members_dev)
     weights = member_weights(heights, cells, values, LBLK, LOC)
     mixing = mixing_matrix(weights, draws)
 

time: 345 us -> 319 us (0.925)
  the two profiles are of different devices: /device:TPU:28 before, /device:TPU:13 now
where the time goes in v1:
time: 319 us; the launch traced here: 317 us
  waiting for transfers between devices  138 us (43%)
  starting transfers between devices  72.7 us (23%)
  local copies, waits for them, and re-layouts  53.2 us (17%)
  matrix products  23.7 us (7%)
  Pallas kernels  18.3 us (6%)
  other arithmetic  10.7 us (3%)
    ppermute x35, waiting for transfers between devices, send_all(): lax.ppermute(pieces[d], axis, shifts(count, d, targets))  136 us
    ppermute x35, starting transfers between devices, send_all(): lax.ppermute(pieces[d], axis, shifts(count, d, targets))  66.6 us
    dynamic_update_slice x16, local copies, waits for them, and re-layouts, put_back(): whole = lax.dynamic_update_slice(whole, piece, (0, field, start, 0))  20.7 us
    slice x26, local copies, waits for them, and re-layouts, hand_back(): updated[d * members_dev:(d + 1) * members_dev]  17.4 us
    dot_general x2, matrix products, merge_fields(): jnp.einsum('rbek,kfrbc->efrbc', mixing, blocks, precision=lax.Precision.H...  15.9 us
    pallas_call x1, Pallas kernels, forecast(): pl.pallas_call(functools.partial(forecast_steps, margin), grid=(members,)...  10.1 us
    pallas_call x1, Pallas kernels, early_heights(): pl.pallas_call(functools.partial(early_kernel, 2 * STEPS), grid=(members,...  8.27 us
    dynamic_slice x3, local copies, waits for them, and re-layouts, row_pieces(): lax.dynamic_slice_in_dim(array, lax.rem(own + d, count) * length, length,...  7.78 us
  transfers between devices with their start and end apart: 37, of which 10 were waited for; matrix products, arithmetic and copies ran while one was open for 26% of the time, Pallas kernels for 3%

profile of v1, /device:TPU:13, one launch (start us, length us, event | category | flops | bytes accessed | tf_op | source)
XLA Modules:
  0.0 317.5 jit_solution(4858672170775975936)
XLA Ops:
  1.5 8.3 %shard_map.55 = f32[8,64,1024]{2,1,0:T(8,128)} custom-call(f32[96,128]{1,0:T(8,128)} %broadcast_in_dim.5.coriolis_ref, f32[8,3,64,1024]{3,2,1,0:T(8,128)} %states_ref.2), custom_call_target="tpu_custom_call" | custom-call | flops 125829120 | bytes 12582912 | tf_op jit(solution)/shard_map/pallas_call | solution.py:110
  9.7 2.8 constant_dynamic-slice_fusion.16
  12.5 3.1 collective-permute-start
  15.7 3.2 %collective-permute-start.1 = (f32[8,8,1024]{2,1,0:T(8,128)}, f32[8,8,1024]{2,1,0:T(8,128)}, u32[]{:S(2)}, u32[]{:S(2)}) collective-permute-start(f32[8,8,1024]{2,1,0:T(8,128)} %get-tuple-element.50), channel_id=1, source_target_pairs={{0,8},{4,12},{8,16},{12,20},{16,24},{28,4},{1,9},{5,13},{9,17},{13... | collective-permute-start | bytes 786440 | tf_op jit(solution)/shard_map/ppermute | solution.py:205
  22.4 3.1 collective-permute-start.8
  25.5 3.0 collective-permute-start.7
  30.1 2.0 collective-permute-done.8.after_ref
  35.4 10.1 %shard_map.56 = (f32[8,64,1024]{2,1,0:T(8,128)}, f32[8,2,64,1024]{3,2,1,0:T(8,128)}) custom-call(f32[2]{0:T(128)} %add_convert_fusion.inside_ref, f32[96,128]{1,0:T(8,128)} %broadcast_in_dim.5.coriolis_ref, f32[8,3,64,1024]{3,2,1,0:T(8,128)} %states_ref.2, f32[8,3,4,1024]{3,2,1,0:T(4,128)} %copy-done.1, f32[8,3,4,1024]{3,2,1,0:T(4,128)} %copy-done), custom_call_target="tpu_custom_call" | custom-call | flops 125829120 | bytes 12582912 | tf_op jit(solution)/shard_map/pallas_call | solution.py:128
  45.5 2.5 constant_dynamic-slice_fusion.8
  48.0 7.8 %collective-permute-start.5 = (f32[8,8,1024]{2,1,0:T(8,128)S(1)}, f32[8,8,1024]{2,1,0:T(8,128)}, u32[]{:S(2)}, u32[]{:S(2)}) collective-permute-start(f32[8,8,1024]{2,1,0:T(8,128)S(1)} %copy-done.3), channel_id=1, source_target_pairs={{0,24},{12,4},{16,8},{20,12},{24,16},{28,20},{1,25},{13,5},{17,9},... | collective-permute-start | bytes 786440 | tf_op jit(solution)/shard_map/ppermute | solution.py:205
  62.0 5.2 %collective-permute-start.12 = (f32[8,8,1024]{2,1,0:T(8,128)S(1)}, f32[8,8,1024]{2,1,0:T(8,128)S(1)}, u32[]{:S(2)}, u32[]{:S(2)}) collective-permute-start(f32[8,8,1024]{2,1,0:T(8,128)S(1)} %get-tuple-element.62), channel_id=1, source_target_pairs={{12,28},{16,0},{13,29},{17,1},{14,30},{18,2},{15,31},{19,3}} | collective-permute-start | bytes 786440 | tf_op jit(solution)/shard_map/ppermute | solution.py:205
  69.9 2.5 constant_dynamic-slice_fusion
  72.5 5.1 %collective-permute-start.23 = (f32[8,2,8,1024]{3,2,1,0:T(8,128)S(1)}, f32[8,2,8,1024]{3,2,1,0:T(8,128)S(1)}, u32[]{:S(2)}, u32[]{:S(2)}) collective-permute-start(f32[8,2,8,1024]{3,2,1,0:T(8,128)S(1)} %get-tuple-element.84), channel_id=1, source_target_pairs={{0,4},{4,8},{8,12},{12,16},{16,20},{20,24},{24,28},{28,0},{1,5},{5... | collective-permute-start | bytes 1572872 | tf_op jit(solution)/shard_map/ppermute | solution.py:205
  77.6 6.1 %collective-permute-start.24 = (f32[8,2,8,1024]{3,2,1,0:T(8,128)S(1)}, f32[8,2,8,1024]{3,2,1,0:T(8,128)S(1)}, u32[]{:S(2)}, u32[]{:S(2)}) collective-permute-start(f32[8,2,8,1024]{3,2,1,0:T(8,128)S(1)} %get-tuple-element.85), channel_id=1, source_target_pairs={{0,8},{4,12},{8,16},{12,20},{16,24},{20,28},{24,0},{28,4},{1,9},{5... | collective-permute-start | bytes 1572872 | tf_op jit(solution)/shard_map/ppermute | solution.py:205
  83.7 6.8 %collective-permute-start.25 = (f32[8,2,8,1024]{3,2,1,0:T(8,128)S(1)}, f32[8,2,8,1024]{3,2,1,0:T(8,128)S(1)}, u32[]{:S(2)}, u32[]{:S(2)}) collective-permute-start(f32[8,2,8,1024]{3,2,1,0:T(8,128)S(1)} %get-tuple-element.86), channel_id=1, source_target_pairs={{0,12},{4,16},{8,20},{12,24},{16,28},{20,0},{24,4},{28,8},{1,13},{... | collective-permute-start | bytes 1572872 | tf_op jit(solution)/shard_map/ppermute | solution.py:205
  99.6 6.8 %fusion.18 = f32[8,64,512]{2,1,0:T(8,128)S(1)} fusion(s32[8,512]{1,0:T(8,128)S(1)} %bitcast.61, f32[64,8,1024]{2,1,0:T(8,128)S(1)} %select_dynamic-update-slice_fusion, f32[8,512]{1,0:T(8,128)S(1)} %bitcast.62), kind=kOutput, calls=%fused_computation.19 | convolution fusion | flops 3225944064 | bytes 3178496 | tf_op jit(solution)/shard_map/erl,rlo->reo/dot_general | solution.py:165
  108.9 6.8 %fusion.12 = f32[64,1,8,8,128]{4,0,3,2,1:T(8,128)S(1)} fusion(f32[64,8,8,128]{3,1,2,0:T(8,128)S(1)} %bitcast.60, s32[8,8,64]{2,1,0:T(8,128)S(1)} %get-tuple-element.134, s32[8,8,64]{2,1,0:T(8,128)S(1)} %get-tuple-element.135, s32[8,8,64]{2,1,0:T(8,128)S(1)} %get-tuple-element.133, f32[8,8,64]{2,1,0:T(8,128)S(1)} %divide_multiply_fusion), kind=kOutput, calls=%fused_computation.15 | convolution fusion | flops 405274624 | bytes 4259840 | tf_op jit(solution)/shard_map/rbek,kfrbc->efrbc/dot_general | solution.py:193
  116.0 3.5 %broadcast_in_dim.4 = f32[8,3,64,1024]{3,2,1,0:T(8,128)} broadcast(f32[]{:T(128)} %constant.108.clone.1), dimensions={} | broadcast | bytes 6291460 | tf_op jit(solution)/shard_map/broadcast_in_dim | solution.py:280
  124.1 2.4 collective-permute-start.28
  127.0 32.5 %collective-permute-done.25 = f32[8,2,8,1024]{3,2,1,0:T(8,128)S(1)} collective-permute-done((f32[8,2,8,1024]{3,2,1,0:T(8,128)S(1)}, f32[8,2,8,1024]{3,2,1,0:T(8,128)S(1)}, u32[]{:S(2)}, u32[]{:S(2)}) %collective-permute-start.25) | collective-permute-done | bytes 524320 | tf_op jit(solution)/shard_map/ppermute | solution.py:205
  159.6 11.3 %collective-permute-done.26 = f32[8,2,8,1024]{3,2,1,0:T(8,128)S(1)} collective-permute-done((f32[8,2,8,1024]{3,2,1,0:T(8,128)S(1)}, f32[8,2,8,1024]{3,2,1,0:T(8,128)S(1)}, u32[]{:S(2)}, u32[]{:S(2)}) %collective-permute-start.26) | collective-permute-done | bytes 524320 | tf_op jit(solution)/shard_map/ppermute | solution.py:205
  171.1 25.3 %collective-permute-done.28 = f32[8,2,8,1024]{3,2,1,0:T(8,128)S(1)} collective-permute-done((f32[8,2,8,1024]{3,2,1,0:T(8,128)S(1)}, f32[8,2,8,1024]{3,2,1,0:T(8,128)S(1)}, u32[]{:S(2)}, u32[]{:S(2)}) %collective-permute-start.28) | collective-permute-done | bytes 524320 | tf_op jit(solution)/shard_map/ppermute | solution.py:205
  196.8 9.1 %fusion.5 = f32[64,2,8,8,128]{4,0,1,3,2:T(8,128)S(1)} fusion(f32[64,2,8,8,128]{4,2,3,1,0:T(8,128)S(1)} %bitcast.59, s32[8,8,64]{2,1,0:T(8,128)S(1)} %get-tuple-element.134, s32[8,8,64]{2,1,0:T(8,128)S(1)} %get-tuple-element.135, s32[8,8,64]{2,1,0:T(8,128)S(1)} %get-tuple-element.133, f32[8,8,64]{2,1,0:T(8,128)S(1)} %divide_multiply_fusion), kind=kOutput, calls=%fused_computation.6 | convolution fusion | flops 807927808 | bytes 8454144 | tf_op jit(solution)/shard_map/rbek,kfrbc->efrbc/dot_general | solution.py:193
  208.2 3.1 collective-permute-start.22
  217.8 2.0 copy.32
  219.9 1.9 slice.137
  226.7 3.3 %collective-permute-start.32 = (f32[8,2,8,1024]{3,2,1,0:T(8,128)}, f32[8,2,8,1024]{3,2,1,0:T(8,128)}, u32[]{:S(2)}, u32[]{:S(2)}) collective-permute-start(f32[8,2,8,1024]{3,2,1,0:T(8,128)} %slice.139), channel_id=1, source_target_pairs={{0,12},{4,16},{8,20},{12,24},{16,28},{20,0},{24,4},{28,8},{1,13},{... | collective-permute-start | bytes 1572872 | tf_op jit(solution)/shard_map/ppermute | solution.py:205
  231.8 26.3 %collective-permute-done.21 = f32[8,1,8,1024]{3,1,2,0:T(1,128)} collective-permute-done((f32[8,1,8,1024]{3,1,2,0:T(1,128)}, f32[8,1,8,1024]{3,1,2,0:T(1,128)}, u32[]{:S(2)}, u32[]{:S(2)}) %collective-permute-start.21) | collective-permute-done | bytes 262176 | tf_op jit(solution)/shard_map/ppermute | solution.py:205
  266.1 2.9 collective-permute-start.36
  270.9 27.1 %collective-permute-done.32 = f32[8,2,8,1024]{3,2,1,0:T(8,128)} collective-permute-done((f32[8,2,8,1024]{3,2,1,0:T(8,128)}, f32[8,2,8,1024]{3,2,1,0:T(8,128)}, u32[]{:S(2)}, u32[]{:S(2)}) %collective-permute-start.32) | collective-permute-done | bytes 524320 | tf_op jit(solution)/shard_map/ppermute | solution.py:205
  299.9 9.4 %collective-permute-done.33 = f32[8,2,8,1024]{3,2,1,0:T(8,128)} collective-permute-done((f32[8,2,8,1024]{3,2,1,0:T(8,128)}, f32[8,2,8,1024]{3,2,1,0:T(8,128)}, u32[]{:S(2)}, u32[]{:S(2)}) %collective-permute-start.33) | collective-permute-done | bytes 524320 | tf_op jit(solution)/shard_map/ppermute | solution.py:205
  312.0 2.4 collective-permute-done.35
  (141 shorter events, 69.3 us)
Async XLA Ops:
  12.5 35.4 %collective-permute-start = (f32[8,8,1024]{2,1,0:T(8,128)}, f32[8,8,1024]{2,1,0:T(8,128)}, u32[]{:S(2)}, u32[]{:S(2)}) collective-permute-start(f32[8,8,1024]{2,1,0:T(8,128)} %get-tuple-element.49), channel_id=1, source_target_pairs={{0,4},{4,8},{8,12},{12,16},{16,20},{20,24},{1,5},{5,9},{9,13},{13,... | collective-permute-start | bytes 786440 | tf_op jit(solution)/shard_map/ppermute | solution.py:205
  15.7 40.1 %collective-permute-start.1 = (f32[8,8,1024]{2,1,0:T(8,128)}, f32[8,8,1024]{2,1,0:T(8,128)}, u32[]{:S(2)}, u32[]{:S(2)}) collective-permute-start(f32[8,8,1024]{2,1,0:T(8,128)} %get-tuple-element.50), channel_id=1, source_target_pairs={{0,8},{4,12},{8,16},{12,20},{16,24},{28,4},{1,9},{5,13},{9,17},{13... | collective-permute-start | bytes 786440 | tf_op jit(solution)/shard_map/ppermute | solution.py:205
  18.9 38.8 %collective-permute-start.2 = (f32[8,8,1024]{2,1,0:T(8,128)}, f32[8,8,1024]{2,1,0:T(8,128)}, u32[]{:S(2)}, u32[]{:S(2)}) collective-permute-start(f32[8,8,1024]{2,1,0:T(8,128)} %get-tuple-element.51), channel_id=1, source_target_pairs={{0,12},{4,16},{8,20},{12,24},{24,4},{28,8},{1,13},{5,17},{9,21},{1... | collective-permute-start | bytes 786440 | tf_op jit(solution)/shard_map/ppermute | solution.py:205
  32.1 27.0 %collective-permute-start.3 = (f32[8,8,1024]{2,1,0:T(8,128)}, f32[8,8,1024]{2,1,0:T(8,128)}, u32[]{:S(2)}, u32[]{:S(2)}) collective-permute-start(f32[8,8,1024]{2,1,0:T(8,128)} %get-tuple-element.52), channel_id=1, source_target_pairs={{0,16},{4,20},{8,24},{20,4},{24,8},{28,12},{1,17},{5,21},{9,25},{2... | collective-permute-start | bytes 786440 | tf_op jit(solution)/shard_map/ppermute | solution.py:205
  34.0 27.3 %collective-permute-start.4 = (f32[8,8,1024]{2,1,0:T(8,128)}, f32[8,8,1024]{2,1,0:T(8,128)}, u32[]{:S(2)}, u32[]{:S(2)}) collective-permute-start(f32[8,8,1024]{2,1,0:T(8,128)} %get-tuple-element.53), channel_id=1, source_target_pairs={{0,20},{4,24},{16,4},{20,8},{24,12},{28,16},{1,21},{5,25},{17,5},{... | collective-permute-start | bytes 786440 | tf_op jit(solution)/shard_map/ppermute | solution.py:205
  48.0 14.0 %collective-permute-start.5 = (f32[8,8,1024]{2,1,0:T(8,128)S(1)}, f32[8,8,1024]{2,1,0:T(8,128)}, u32[]{:S(2)}, u32[]{:S(2)}) collective-permute-start(f32[8,8,1024]{2,1,0:T(8,128)S(1)} %copy-done.3), channel_id=1, source_target_pairs={{0,24},{12,4},{16,8},{20,12},{24,16},{28,20},{1,25},{13,5},{17,9},... | collective-permute-start | bytes 786440 | tf_op jit(solution)/shard_map/ppermute | solution.py:205
  55.8 11.4 %collective-permute-start.6 = (f32[8,8,1024]{2,1,0:T(8,128)S(1)}, f32[8,8,1024]{2,1,0:T(8,128)}, u32[]{:S(2)}, u32[]{:S(2)}) collective-permute-start(f32[8,8,1024]{2,1,0:T(8,128)S(1)} %copy-done.2), channel_id=1, source_target_pairs={{8,4},{12,8},{16,12},{20,16},{24,20},{28,24},{9,5},{13,9},{17,13},... | collective-permute-start | bytes 786440 | tf_op jit(solution)/shard_map/ppermute | solution.py:205
  62.0 15.6 %collective-permute-start.12 = (f32[8,8,1024]{2,1,0:T(8,128)S(1)}, f32[8,8,1024]{2,1,0:T(8,128)S(1)}, u32[]{:S(2)}, u32[]{:S(2)}) collective-permute-start(f32[8,8,1024]{2,1,0:T(8,128)S(1)} %get-tuple-element.62), channel_id=1, source_target_pairs={{12,28},{16,0},{13,29},{17,1},{14,30},{18,2},{15,31},{19,3}} | collective-permute-start | bytes 786440 | tf_op jit(solution)/shard_map/ppermute | solution.py:205
  67.2 16.5 %collective-permute-start.13 = (f32[8,8,1024]{2,1,0:T(8,128)S(1)}, f32[8,8,1024]{2,1,0:T(8,128)S(1)}, u32[]{:S(2)}, u32[]{:S(2)}) collective-permute-start(f32[8,8,1024]{2,1,0:T(8,128)S(1)} %get-tuple-element.63), channel_id=1, source_target_pairs={{8,28},{12,0},{9,29},{13,1},{10,30},{14,2},{11,31},{15,3}} | collective-permute-start | bytes 786440 | tf_op jit(solution)/shard_map/ppermute | solution.py:205
  68.5 21.9 %collective-permute-start.14 = (f32[8,8,1024]{2,1,0:T(8,128)S(1)}, f32[8,8,1024]{2,1,0:T(8,128)S(1)}, u32[]{:S(2)}, u32[]{:S(2)}) collective-permute-start(f32[8,8,1024]{2,1,0:T(8,128)S(1)} %get-tuple-element.64), channel_id=1, source_target_pairs={{4,28},{8,0},{5,29},{9,1},{6,30},{10,2},{7,31},{11,3}} | collective-permute-start | bytes 786440 | tf_op jit(solution)/shard_map/ppermute | solution.py:205
  69.2 22.6 %collective-permute-start.15 = (f32[8,8,1024]{2,1,0:T(8,128)S(1)}, f32[8,8,1024]{2,1,0:T(8,128)S(1)}, u32[]{:S(2)}, u32[]{:S(2)}) collective-permute-start(f32[8,8,1024]{2,1,0:T(8,128)S(1)} %get-tuple-element.65), channel_id=1, source_target_pairs={{0,28},{4,0},{1,29},{5,1},{2,30},{6,2},{3,31},{7,3}} | collective-permute-start | bytes 786440 | tf_op jit(solution)/shard_map/ppermute | solution.py:205
  72.5 51.6 %collective-permute-start.23 = (f32[8,2,8,1024]{3,2,1,0:T(8,128)S(1)}, f32[8,2,8,1024]{3,2,1,0:T(8,128)S(1)}, u32[]{:S(2)}, u32[]{:S(2)}) collective-permute-start(f32[8,2,8,1024]{3,2,1,0:T(8,128)S(1)} %get-tuple-element.84), channel_id=1, source_target_pairs={{0,4},{4,8},{8,12},{12,16},{16,20},{20,24},{24,28},{28,0},{1,5},{5... | collective-permute-start | bytes 1572872 | tf_op jit(solution)/shard_map/ppermute | solution.py:205
  77.6 48.9 %collective-permute-start.24 = (f32[8,2,8,1024]{3,2,1,0:T(8,128)S(1)}, f32[8,2,8,1024]{3,2,1,0:T(8,128)S(1)}, u32[]{:S(2)}, u32[]{:S(2)}) collective-permute-start(f32[8,2,8,1024]{3,2,1,0:T(8,128)S(1)} %get-tuple-element.85), channel_id=1, source_target_pairs={{0,8},{4,12},{8,16},{12,20},{16,24},{20,28},{24,0},{28,4},{1,9},{5... | collective-permute-start | bytes 1572872 | tf_op jit(solution)/shard_map/ppermute | solution.py:205
  83.7 75.9 %collective-permute-start.25 = (f32[8,2,8,1024]{3,2,1,0:T(8,128)S(1)}, f32[8,2,8,1024]{3,2,1,0:T(8,128)S(1)}, u32[]{:S(2)}, u32[]{:S(2)}) collective-permute-start(f32[8,2,8,1024]{3,2,1,0:T(8,128)S(1)} %get-tuple-element.86), channel_id=1, source_target_pairs={{0,12},{4,16},{8,20},{12,24},{16,28},{20,0},{24,4},{28,8},{1,13},{... | collective-permute-start | bytes 1572872 | tf_op jit(solution)/shard_map/ppermute | solution.py:205
  90.5 80.4 %collective-permute-start.26 = (f32[8,2,8,1024]{3,2,1,0:T(8,128)S(1)}, f32[8,2,8,1024]{3,2,1,0:T(8,128)S(1)}, u32[]{:S(2)}, u32[]{:S(2)}) collective-permute-start(f32[8,2,8,1024]{3,2,1,0:T(8,128)S(1)} %get-tuple-element.87), channel_id=1, source_target_pairs={{0,16},{4,20},{8,24},{12,28},{16,0},{20,4},{24,8},{28,12},{1,17},{... | collective-permute-start | bytes 1572872 | tf_op jit(solution)/shard_map/ppermute | solution.py:205
  91.9 79.1 %collective-permute-start.27 = (f32[8,2,8,1024]{3,2,1,0:T(8,128)S(1)}, f32[8,2,8,1024]{3,2,1,0:T(8,128)S(1)}, u32[]{:S(2)}, u32[]{:S(2)}) collective-permute-start(f32[8,2,8,1024]{3,2,1,0:T(8,128)S(1)} %get-tuple-element.88), channel_id=1, source_target_pairs={{0,20},{4,24},{8,28},{12,0},{16,4},{20,8},{24,12},{28,16},{1,21},{... | collective-permute-start | bytes 1572872 | tf_op jit(solution)/shard_map/ppermute | solution.py:205
  124.1 72.2 %collective-permute-start.28 = (f32[8,2,8,1024]{3,2,1,0:T(8,128)S(1)}, f32[8,2,8,1024]{3,2,1,0:T(8,128)S(1)}, u32[]{:S(2)}, u32[]{:S(2)}) collective-permute-start(f32[8,2,8,1024]{3,2,1,0:T(8,128)S(1)} %get-tuple-element.89), channel_id=1, source_target_pairs={{0,24},{4,28},{8,0},{12,4},{16,8},{20,12},{24,16},{28,20},{1,25},{... | collective-permute-start | bytes 1572872 | tf_op jit(solution)/shard_map/ppermute | solution.py:205
  126.5 70.2 %collective-permute-start.29 = (f32[8,2,8,1024]{3,2,1,0:T(8,128)S(1)}, f32[8,2,8,1024]{3,2,1,0:T(8,128)S(1)}, u32[]{:S(2)}, u32[]{:S(2)}) collective-permute-start(f32[8,2,8,1024]{3,2,1,0:T(8,128)S(1)} %get-tuple-element.90), channel_id=1, source_target_pairs={{0,28},{4,0},{8,4},{12,8},{16,12},{20,16},{24,20},{28,24},{1,29},{... | collective-permute-start | bytes 1572872 | tf_op jit(solution)/shard_map/ppermute | solution.py:205
  159.6 47.7 %collective-permute-start.16 = (f32[8,1,8,1024]{3,1,2,0:T(1,128)S(1)}, f32[8,1,8,1024]{3,1,2,0:T(1,128)S(1)}, u32[]{:S(2)}, u32[]{:S(2)}) collective-permute-start(f32[8,1,8,1024]{3,1,2,0:T(1,128)S(1)} %bitcast.58), channel_id=1, source_target_pairs={{0,4},{4,8},{8,12},{12,16},{16,20},{20,24},{24,28},{28,0},{1,5},{5... | collective-permute-start | bytes 786440 | tf_op jit(solution)/shard_map/ppermute | solution.py:205
  170.9 37.3 %collective-permute-start.17 = (f32[8,1,8,1024]{3,1,2,0:T(1,128)S(1)}, f32[8,1,8,1024]{3,1,2,0:T(1,128)S(1)}, u32[]{:S(2)}, u32[]{:S(2)}) collective-permute-start(f32[8,1,8,1024]{3,1,2,0:T(1,128)S(1)} %bitcast.57), channel_id=1, source_target_pairs={{0,8},{4,12},{8,16},{12,20},{16,24},{20,28},{24,0},{28,4},{1,9},{5... | collective-permute-start | bytes 786440 | tf_op jit(solution)/shard_map/ppermute | solution.py:205
  170.9 44.0 %collective-permute-start.18 = (f32[8,1,8,1024]{3,1,2,0:T(1,128)}, f32[8,1,8,1024]{3,1,2,0:T(1,128)}, u32[]{:S(2)}, u32[]{:S(2)}) collective-permute-start(f32[8,1,8,1024]{3,1,2,0:T(1,128)} %bitcast.14), channel_id=1, source_target_pairs={{0,12},{4,16},{8,20},{12,24},{16,28},{20,0},{24,4},{28,8},{1,13},{... | collective-permute-start | bytes 786440 | tf_op jit(solution)/shard_map/ppermute | solution.py:205
  196.3 25.5 %collective-permute-start.19 = (f32[8,1,8,1024]{3,1,2,0:T(1,128)}, f32[8,1,8,1024]{3,1,2,0:T(1,128)}, u32[]{:S(2)}, u32[]{:S(2)}) collective-permute-start(f32[8,1,8,1024]{3,1,2,0:T(1,128)} %bitcast.15), channel_id=1, source_target_pairs={{0,16},{4,20},{8,24},{12,28},{16,0},{20,4},{24,8},{28,12},{1,17},{... | collective-permute-start | bytes 786440 | tf_op jit(solution)/shard_map/ppermute | solution.py:205
  196.7 30.0 %collective-permute-start.20 = (f32[8,1,8,1024]{3,1,2,0:T(1,128)}, f32[8,1,8,1024]{3,1,2,0:T(1,128)S(1)}, u32[]{:S(2)}, u32[]{:S(2)}) collective-permute-start(f32[8,1,8,1024]{3,1,2,0:T(1,128)} %bitcast.16), channel_id=1, source_target_pairs={{0,20},{4,24},{8,28},{12,0},{16,4},{20,8},{24,12},{28,16},{1,21},{... | collective-permute-start | bytes 786440 | tf_op jit(solution)/shard_map/ppermute | solution.py:205
  207.3 50.8 %collective-permute-start.21 = (f32[8,1,8,1024]{3,1,2,0:T(1,128)}, f32[8,1,8,1024]{3,1,2,0:T(1,128)}, u32[]{:S(2)}, u32[]{:S(2)}) collective-permute-start(f32[8,1,8,1024]{3,1,2,0:T(1,128)} %bitcast.17), channel_id=1, source_target_pairs={{0,24},{4,28},{8,0},{12,4},{16,8},{20,12},{24,16},{28,20},{1,25},{... | collective-permute-start | bytes 786440 | tf_op jit(solution)/shard_map/ppermute | solution.py:205
  208.2 52.2 %collective-permute-start.22 = (f32[8,1,8,1024]{3,1,2,0:T(1,128)}, f32[8,1,8,1024]{3,1,2,0:T(1,128)}, u32[]{:S(2)}, u32[]{:S(2)}) collective-permute-start(f32[8,1,8,1024]{3,1,2,0:T(1,128)} %bitcast.18), channel_id=1, source_target_pairs={{0,28},{4,0},{8,4},{12,8},{16,12},{20,16},{24,20},{28,24},{1,29},{... | collective-permute-start | bytes 786440 | tf_op jit(solution)/shard_map/ppermute | solution.py:205
  214.9 48.6 %collective-permute-start.30 = (f32[8,2,8,1024]{3,2,1,0:T(8,128)}, f32[8,2,8,1024]{3,2,1,0:T(8,128)}, u32[]{:S(2)}, u32[]{:S(2)}) collective-permute-start(f32[8,2,8,1024]{3,2,1,0:T(8,128)} %slice.135), channel_id=1, source_target_pairs={{0,4},{4,8},{8,12},{12,16},{16,20},{20,24},{24,28},{28,0},{1,5},{5... | collective-permute-start | bytes 1572872 | tf_op jit(solution)/shard_map/ppermute | solution.py:205
  221.8 44.3 %collective-permute-start.31 = (f32[8,2,8,1024]{3,2,1,0:T(8,128)}, f32[8,2,8,1024]{3,2,1,0:T(8,128)}, u32[]{:S(2)}, u32[]{:S(2)}) collective-permute-start(f32[8,2,8,1024]{3,2,1,0:T(8,128)} %slice.137), channel_id=1, source_target_pairs={{0,8},{4,12},{8,16},{12,20},{16,24},{20,28},{24,0},{28,4},{1,9},{5... | collective-permute-start | bytes 1572872 | tf_op jit(solution)/shard_map/ppermute | solution.py:205
  226.7 71.4 %collective-permute-start.32 = (f32[8,2,8,1024]{3,2,1,0:T(8,128)}, f32[8,2,8,1024]{3,2,1,0:T(8,128)}, u32[]{:S(2)}, u32[]{:S(2)}) collective-permute-start(f32[8,2,8,1024]{3,2,1,0:T(8,128)} %slice.139), channel_id=1, source_target_pairs={{0,12},{4,16},{8,20},{12,24},{16,28},{20,0},{24,4},{28,8},{1,13},{... | collective-permute-start | bytes 1572872 | tf_op jit(solution)/shard_map/ppermute | solution.py:205
  258.1 51.1 %collective-permute-start.33 = (f32[8,2,8,1024]{3,2,1,0:T(8,128)}, f32[8,2,8,1024]{3,2,1,0:T(8,128)}, u32[]{:S(2)}, u32[]{:S(2)}) collective-permute-start(f32[8,2,8,1024]{3,2,1,0:T(8,128)} %slice.141), channel_id=1, source_target_pairs={{0,16},{4,20},{8,24},{12,28},{16,0},{20,4},{24,8},{28,12},{1,17},{... | collective-permute-start | bytes 1572872 | tf_op jit(solution)/shard_map/ppermute | solution.py:205
  260.4 50.8 %collective-permute-start.34 = (f32[8,2,8,1024]{3,2,1,0:T(8,128)S(1)}, f32[8,2,8,1024]{3,2,1,0:T(8,128)S(1)}, u32[]{:S(2)}, u32[]{:S(2)}) collective-permute-start(f32[8,2,8,1024]{3,2,1,0:T(8,128)S(1)} %slice.143), channel_id=1, source_target_pairs={{0,20},{4,24},{8,28},{12,0},{16,4},{20,8},{24,12},{28,16},{1,21},{... | collective-permute-start | bytes 1572872 | tf_op jit(solution)/shard_map/ppermute | solution.py:205
  263.5 50.8 %collective-permute-start.35 = (f32[8,2,8,1024]{3,2,1,0:T(8,128)S(1)}, f32[8,2,8,1024]{3,2,1,0:T(8,128)S(1)}, u32[]{:S(2)}, u32[]{:S(2)}) collective-permute-start(f32[8,2,8,1024]{3,2,1,0:T(8,128)S(1)} %slice.145), channel_id=1, source_target_pairs={{0,24},{4,28},{8,0},{12,4},{16,8},{20,12},{24,16},{28,20},{1,25},{... | collective-permute-start | bytes 1572872 | tf_op jit(solution)/shard_map/ppermute | solution.py:205
  266.1 50.6 %collective-permute-start.36 = (f32[8,2,8,1024]{3,2,1,0:T(8,128)S(1)}, f32[8,2,8,1024]{3,2,1,0:T(8,128)S(1)}, u32[]{:S(2)}, u32[]{:S(2)}) collective-permute-start(f32[8,2,8,1024]{3,2,1,0:T(8,128)S(1)} %slice.147), channel_id=1, source_target_pairs={{0,28},{4,0},{8,4},{12,8},{16,12},{20,16},{24,20},{28,24},{1,29},{... | collective-permute-start | bytes 1572872 | tf_op jit(solution)/shard_map/ppermute | solution.py:205
  (14 other events, 193.3 us)

commit v2 on v1

--- a/solution.py
+++ b/solution.py
@@ -33,16 +33,8 @@
     return before, after
 
 
-def early_kernel(margin, coriolis_ref, states_ref, height_ref, here, there):
-    forecast_steps(margin, None, coriolis_ref, states_ref, None, None, height_ref, None, here, there)
-
-
-def forecast_steps(margin, inside_ref, coriolis_ref, states_ref, before_ref, after_ref,
-                   height_ref, winds_ref, here, there):
-    rows, width = states_ref.shape[2:]
-    last = rows // SUBLANES + 2
-    first_row = 2 * SUBLANES
-    with_halo = before_ref is not None
+def forecast_steps(here, there, tiles, final, masked, factor):
+    width = here.shape[2]
 
     def tile(t, shift=0):
         return slice(t * SUBLANES + shift, (t + 1) * SUBLANES + shift)
@@ -53,99 +45,141 @@
     def north(ref, field, t):
         return ref[field, tile(t, 1), :] - ref[field, tile(t, -1), :]
 
-    def masked(quantity, t):
-        if t == 1:
-            return quantity * inside_ref[0]
-        if t == last:
-            return quantity * inside_ref[1]
-        return quantity
-
-    here[:, first_row : first_row + rows, :] = states_ref[0]
-    if with_halo:
-        here[:, first_row - margin : first_row, :] = before_ref[0]
-        here[:, first_row + rows : first_row + rows + margin, :] = after_ref[0]
     old, new = here, there
     for step in range(STEPS):
-        final = step == STEPS - 1
-        for t in range(1, last + 1) if with_halo else range(2, last):
+        for t in tiles:
             slope = east(old[1, tile(t), :]) + north(old, 2, t)
-            height = masked(old[0, tile(t), :] - (0.5 * FLOW_FACTOR) * slope, t)
-            new[0, tile(t), :] = height
-            if final and 1 < t < last:
-                height_ref[0, tile(t - 2), :] = height
-        if final and winds_ref is None:
-            break
-        for t in range(1, last + 1) if with_halo and not final else range(2, last):
-            factor = jnp.concatenate([coriolis_ref[tile(t), :]] * (width // LANES), axis=1)
+            new[0, tile(t), :] = masked(
+                old[0, tile(t), :] - (0.5 * FLOW_FACTOR) * slope, t
+            )
+        for t in final if step == STEPS - 1 else tiles:
+            turn = factor(t)
             east_old, north_old = old[1, tile(t), :], old[2, tile(t), :]
             east_new = (
-                east_old - (0.5 * PRESSURE_FACTOR) * east(new[0, tile(t), :]) + factor * north_old
+                east_old - (0.5 * PRESSURE_FACTOR) * east(new[0, tile(t), :]) + turn * north_old
             )
-            north_new = north_old - (0.5 * PRESSURE_FACTOR) * north(new, 0, t) - factor * east_old
-            if final:
-                winds_ref[0, 0, tile(t - 2), :] = east_new
-                winds_ref[0, 1, tile(t - 2), :] = north_new
-            else:
-                new[1, tile(t), :] = masked(east_new, t)
-                new[2, tile(t), :] = masked(north_new, t)
+            north_new = north_old - (0.5 * PRESSURE_FACTOR) * north(new, 0, t) - turn * east_old
+            new[1, tile(t), :] = masked(east_new, t)
+            new[2, tile(t), :] = masked(north_new, t)
         old, new = new, old
+    return old
+
+
+def coriolis_tile(coriolis_ref, t, width):
+    factors = coriolis_ref[t * SUBLANES : (t + 1) * SUBLANES, :]
+    return jnp.concatenate([factors] * (width // LANES), axis=1)
+
+
+def early_kernel(count, place_ref, coriolis_ref, states_ref, *refs):
+    rows, width = states_ref.shape[2:]
+    outs, (here, there) = refs[:-2], refs[-2:]
+    first = 2 * SUBLANES
+    tiles = range(2, rows // SUBLANES + 2)
+    here[:, first : first + rows, :] = states_ref[0]
+    done = forecast_steps(
+        here, there, tiles, tiles,
+        lambda quantity, t: quantity,
+        lambda t: coriolis_tile(coriolis_ref, t, width),
+    )
+    if len(outs) == 2:
+        outs[0][0] = done[0, first : first + rows, :]
+        outs[1][0] = done[1:, first : first + rows, :]
+        return
+    piece = rows // count
+    for d in range(count):
+        start = pl.multiple_of(lax.rem(place_ref[0] + d, count) * piece, SUBLANES)
+        outs[d][0] = done[0, pl.ds(first + start, piece), :]
+        outs[count + d][0] = done[1:, pl.ds(first + start, piece), :]
+
+
+def edge_kernel(inside_ref, coriolis_ref, low_ref, high_ref, before_ref, after_ref,
+                height_ref, winds_ref, here, there):
+    margin, width = before_ref.shape[2:]
+    last_tile = coriolis_ref.shape[0] // SUBLANES - 5
+    for edge in range(2):
+        if edge == 0:
+            here[:, 2 * SUBLANES - margin : 2 * SUBLANES, :] = before_ref[0]
+            here[:, 2 * SUBLANES : 4 * SUBLANES, :] = low_ref[0]
+        else:
+            here[:, SUBLANES : 3 * SUBLANES, :] = high_ref[0]
+            here[:, 3 * SUBLANES : 3 * SUBLANES + margin, :] = after_ref[0]
+        outside = 1 if edge == 0 else 3
+        shift = 0 if edge == 0 else last_tile
+        done = forecast_steps(
+            here, there, (1, 2, 3), (2,),
+            lambda quantity, t: quantity * inside_ref[edge] if t == outside else quantity,
+            lambda t: coriolis_tile(coriolis_ref, t + shift, width),
+        )
+        rows = slice(edge * SUBLANES, (edge + 1) * SUBLANES)
+        height_ref[0, rows, :] = done[0, 2 * SUBLANES : 3 * SUBLANES, :]
+        winds_ref[0, :, rows, :] = done[1:, 2 * SUBLANES : 3 * SUBLANES, :]
 
 
 def coriolis_frame(coriolis, band_index, rows):
-    frame = rows + 4 * SUBLANES
-    factors = lax.dynamic_slice_in_dim(
-        jnp.pad(coriolis, (2 * SUBLANES, 2 * SUBLANES)), band_index * rows, frame
-    )
-    return jnp.broadcast_to(factors[:, None], (frame, LANES))
-
-
-def forecast_cost(states):
-    return pl.CostEstimate(
-        flops=40 * states.size * STEPS, bytes_accessed=8 * states.size, transcendentals=0
-    )
-
-
-def early_heights(states, factors):
+    padded = jnp.pad(coriolis, (2 * SUBLANES, 2 * SUBLANES))
+    spread = jnp.broadcast_to(padded[:, None], padded.shape + (LANES,))
+    return lax.dynamic_slice_in_dim(spread, band_index * rows, rows + 4 * SUBLANES)
+
+
+def forecast_cost(states, rows):
+    size = states.size * rows // states.shape[2]
+    return pl.CostEstimate(flops=40 * size * STEPS, bytes_accessed=8 * size, transcendentals=0)
+
+
+def early_pieces(states, factors, axis):
     members, fields, rows, width = states.shape
-    return pl.pallas_call(
-        functools.partial(early_kernel, 2 * STEPS),
-        grid=(members,),
-        in_specs=[
-            pl.BlockSpec(factors.shape, lambda m: (0, 0)),
-            pl.BlockSpec((1, fields, rows, width), lambda m: (m, 0, 0, 0)),
-        ],
-        out_specs=pl.BlockSpec((1, rows, width), lambda m: (m, 0, 0)),
-        out_shape=jax.ShapeDtypeStruct((members, rows, width), jnp.float32),
-        scratch_shapes=[pltpu.VMEM((fields, factors.shape[0], width), jnp.float32)] * 2,
-        cost_estimate=forecast_cost(states),
-    )(factors, states)
-
-
-def forecast(states, before, after, factors, band_index, band_count):
-    members, fields, rows, width = states.shape
-    margin = 2 * STEPS
-    inside = jnp.stack([band_index > 0, band_index < band_count - 1]).astype(jnp.float32)
-    return pl.pallas_call(
-        functools.partial(forecast_steps, margin),
+    count = lax.axis_size(axis)
+    piece = rows // count
+    whole = piece % SUBLANES != 0
+    heights, winds = (rows,) if whole else (piece,) * count, (rows,) if whole else (piece,) * count
+    place = lax.axis_index(axis).astype(jnp.int32).reshape(1)
+    found = pl.pallas_call(
+        functools.partial(early_kernel, count),
         grid=(members,),
         in_specs=[
             pl.BlockSpec(memory_space=pltpu.SMEM),
             pl.BlockSpec(factors.shape, lambda m: (0, 0)),
             pl.BlockSpec((1, fields, rows, width), lambda m: (m, 0, 0, 0)),
+        ],
+        out_specs=[pl.BlockSpec((1, r, width), lambda m: (m, 0, 0)) for r in heights]
+        + [pl.BlockSpec((1, fields - 1, r, width), lambda m: (m, 0, 0, 0)) for r in winds],
+        out_shape=[jax.ShapeDtypeStruct((members, r, width), jnp.float32) for r in heights]
+        + [jax.ShapeDtypeStruct((members, fields - 1, r, width), jnp.float32) for r in winds],
+        scratch_shapes=[pltpu.VMEM((fields, factors.shape[0], width), jnp.float32)] * 2,
+        cost_estimate=forecast_cost(states, rows),
+    )(place, factors, states)
+    if whole:
+        return row_pieces(found[0], axis, 1), row_pieces(found[1], axis, 2)
+    return list(found[:count]), list(found[count:])
+
+
+def edge_forecast(states, before, after, factors, band_index, band_count):
+    members, fields, rows, width = states.shape
+    margin = 2 * STEPS
+    inside = jnp.stack([band_index > 0, band_index < band_count - 1]).astype(jnp.float32)
+    last = rows // (2 * SUBLANES) - 1
+    return pl.pallas_call(
+        edge_kernel,
+        grid=(members,),
+        in_specs=[
+            pl.BlockSpec(memory_space=pltpu.SMEM),
+            pl.BlockSpec(factors.shape, lambda m: (0, 0)),
+            pl.BlockSpec((1, fields, 2 * SUBLANES, width), lambda m: (m, 0, 0, 0)),
+            pl.BlockSpec((1, fields, 2 * SUBLANES, width), lambda m: (m, 0, last, 0)),
             pl.BlockSpec((1, fields, margin, width), lambda m: (m, 0, 0, 0)),
             pl.BlockSpec((1, fields, margin, width), lambda m: (m, 0, 0, 0)),
         ],
         out_specs=[
-            pl.BlockSpec((1, rows, width), lambda m: (m, 0, 0)),
-            pl.BlockSpec((1, fields - 1, rows, width), lambda m: (m, 0, 0, 0)),
+            pl.BlockSpec((1, 2 * SUBLANES, width), lambda m: (m, 0, 0)),
+            pl.BlockSpec((1, fields - 1, 2 * SUBLANES, width), lambda m: (m, 0, 0, 0)),
         ],
         out_shape=[
-            jax.ShapeDtypeStruct((members, rows, width), jnp.float32),
-            jax.ShapeDtypeStruct((members, fields - 1, rows, width), jnp.float32),
+            jax.ShapeDtypeStruct((members, 2 * SUBLANES, width), jnp.float32),
+            jax.ShapeDtypeStruct((members, fields - 1, 2 * SUBLANES, width), jnp.float32),
         ],
-        scratch_shapes=[pltpu.VMEM((fields, factors.shape[0], width), jnp.float32)] * 2,
-        cost_estimate=forecast_cost(states),
-    )(inside, factors, states, before, after)
+        scratch_shapes=[pltpu.VMEM((fields, 5 * SUBLANES, width), jnp.float32)] * 2,
+        cost_estimate=forecast_cost(states, 6 * SUBLANES),
+    )(inside, factors, states, states, before, after)
 
 
 def tapering(cells, grid_width, block_cells, length):
@@ -198,12 +232,17 @@
     return [(i, (i + d) % count) for i in range(count) if (i + d) % count in targets]
 
 
+def by_reach(count):
+    return sorted(range(1, count), key=lambda d: abs(2 * d - count))
+
+
 def send_all(pieces, axis, targets=None):
     count = lax.axis_size(axis)
     targets = range(count) if targets is None else targets
-    return pieces[:1] + [
-        lax.ppermute(pieces[d], axis, shifts(count, d, targets)) for d in range(1, count)
-    ]
+    received = {0: pieces[0]}
+    for d in by_reach(count):
+        received[d] = lax.ppermute(pieces[d], axis, shifts(count, d, targets))
+    return [received[d] for d in range(count)]
 
 
 def row_pieces(array, axis, dim):
@@ -214,6 +253,18 @@
         lax.dynamic_slice_in_dim(array, lax.rem(own + d, count) * length, length, axis=dim)
         for d in range(count)
     ]
+    return lax.optimization_barrier(pieces)
+
+
+def edge_pieces(array, axis, dim, length):
+    count = lax.axis_size(axis)
+    own = lax.axis_index(axis)
+    held = array.shape[dim]
+    pieces = []
+    for d in range(count):
+        owner = lax.rem(own + d, count)
+        start = jnp.where(2 * owner < count, owner * length, held - (count - owner) * length)
+        pieces.append(lax.dynamic_slice_in_dim(array, start, length, axis=dim))
     return lax.optimization_barrier(pieces)
 
 
@@ -252,19 +303,26 @@
     outer = [j for j in range(count) if j not in inner]
     factors = coriolis_frame(coriolis, band_index, count_of_rows)
 
-    first = row_pieces(early_heights(particle_states, factors), "mem", 1)
-    inner_heights = send_all(first, "mem", inner)
-    states, _ = lax.optimization_barrier((particle_states, first))
+    heights, winds = early_pieces(particle_states, factors, "mem")
+    inner_heights = send_all(heights, "mem", inner)
+    states, heights = lax.optimization_barrier((particle_states, heights))
     before, after = edge_rows(states, "dom", 2, margin)
-    height, winds = forecast(states, before, after, factors, band_index, lax.axis_size("dom"))
-    outer_heights = send_all(row_pieces(height, "mem", 1), "mem", outer)
-    winds_all = send_all(row_pieces(winds, "mem", 2), "mem")
+    inner_winds = send_all(winds, "mem", inner)
+    edges = edge_forecast(
+        states, before, after, factors, band_index, lax.axis_size("dom")
+    )
+    outer_heights = send_all(edge_pieces(edges[0], "mem", 1, piece), "mem", outer)
+    outer_winds = send_all(edge_pieces(edges[1], "mem", 2, piece), "mem", outer)
     inner_heights, outer_heights = lax.optimization_barrier((inner_heights, outer_heights))
     is_outer = jnp.any(jnp.stack([own == j for j in outer]))
-    heights = jnp.concatenate(
-        [jnp.where(is_outer, a, b) for a, b in zip(outer_heights, inner_heights)], axis=0
-    )
-    winds_all = jnp.concatenate(winds_all, axis=0)
+
+    def gather(at_edge, within):
+        return jnp.concatenate(
+            [jnp.where(is_outer, a, b) for a, b in zip(at_edge, within)], axis=0
+        )
+
+    heights = gather(outer_heights, inner_heights)
+    winds_all = gather(outer_winds, inner_winds)
 
     cells = observed_cells[0]
     values = observed_values[0]

time: 319 us -> 343 us (1.075)
  the two profiles are of different devices: /device:TPU:13 before, /device:TPU:28 now
where the time goes in v2:
time: 343 us; the launch traced here: 341 us
  starting transfers between devices  160 us (47%)
  waiting for transfers between devices  83.6 us (24%)
  local copies, waits for them, and re-layouts  47.6 us (14%)
  matrix products  23.7 us (7%)
  Pallas kernels  18.8 us (5%)
  other arithmetic  5.95 us (2%)
    ppermute x42, starting transfers between devices, send_all(): received[d] = lax.ppermute(pieces[d], axis, shifts(count, d, targets))  156 us
    ppermute x42, waiting for transfers between devices, send_all(): received[d] = lax.ppermute(pieces[d], axis, shifts(count, d, targets))  83.6 us
    dynamic_update_slice x16, local copies, waits for them, and re-layouts, put_back(): whole = lax.dynamic_update_slice(whole, piece, (0, field, start, 0))  20.7 us
    slice x26, local copies, waits for them, and re-layouts, hand_back(): updated[d * members_dev:(d + 1) * members_dev]  17.4 us
    dot_general x2, matrix products, merge_fields(): jnp.einsum('rbek,kfrbc->efrbc', mixing, blocks, precision=lax.Precision.H...  15.9 us
    pallas_call x1, Pallas kernels, early_pieces(): pl.pallas_call(functools.partial(early_kernel, count), grid=(members,), i...  9.75 us
    pallas_call x1, Pallas kernels, edge_forecast(): pl.pallas_call(edge_kernel, grid=(members,), in_specs=[pl.BlockSpec(memor...  9.02 us
  transfers between devices with their start and end apart: 44, of which 8 were waited for; matrix products, arithmetic and copies ran while one was open for 22% of the time, Pallas kernels for 3%

profile of v2, /device:TPU:28, one launch (start us, length us, event | category | flops | bytes accessed | tf_op | source)
XLA Modules:
  0.0 340.8 jit_solution(13480969910854364795)
XLA Ops:
  1.5 9.7 %shard_map.55 = (f32[8,8,1024]{2,1,0:T(8,128)}, f32[8,8,1024]{2,1,0:T(8,128)}, f32[8,8,1024]{2,1,0:T(8,128)}, f32[8,8,1024]{2,1,0:T(8,128)}, f32[8,8,1024]{2,1,0...) custom-call(s32[1]{0:T(128)} %bitcast.place_ref, ...), custom_call_target="tpu_custom_call" | custom-call | flops 125829120 | bytes 12582912 | tf_op jit(solution)/shard_map/pallas_call | solution.py:136
  11.9 5.6 %collective-permute-start.1 = (f32[8,8,1024]{2,1,0:T(8,128)}, f32[8,8,1024]{2,1,0:T(8,128)}, u32[]{:S(2)}, u32[]{:S(2)}) collective-permute-start(f32[8,8,1024]{2,1,0:T(8,128)} %get-tuple-element.58), channel_id=1, source_target_pairs={{0,8},{4,12},{8,16},{12,20},{16,24},{28,4},{1,9},{5,13},{9,17},{13... | collective-permute-start | bytes 786440 | tf_op jit(solution)/shard_map/ppermute | solution.py:244
  17.5 3.5 %collective-permute-start.2 = (f32[8,8,1024]{2,1,0:T(8,128)}, f32[8,8,1024]{2,1,0:T(8,128)}, u32[]{:S(2)}, u32[]{:S(2)}) collective-permute-start(f32[8,8,1024]{2,1,0:T(8,128)} %get-tuple-element.59), channel_id=1, source_target_pairs={{0,12},{4,16},{8,20},{12,24},{24,4},{28,8},{1,13},{5,17},{9,21},{1... | collective-permute-start | bytes 786440 | tf_op jit(solution)/shard_map/ppermute | solution.py:244
  23.9 3.1 collective-permute-start.7
  28.9 2.0 collective-permute-start.3
  33.5 9.0 %shard_map.56 = (f32[8,16,1024]{2,1,0:T(8,128)}, f32[8,2,16,1024]{3,2,1,0:T(8,128)}) custom-call(f32[2]{0:T(128)} %add_convert_fusion.inside_ref, f32[96,128]{1,0:T(8,128)} %broadcast_in_dim.5.coriolis_ref, f32[8,3,64,1024]{3,2,1,0:T(8,128)} %high_ref, f32[8,3,64,1024]{3,2,1,0:T(8,128)} %high_ref, f32[8,3,4,1024]{3,2,1,0:T(4,128)} %copy-done.3, ...), custom_call_target="tpu_custom_call" | custom-call | flops 94371840 | bytes 9437184 | tf_op jit(solution)/shard_map/pallas_call | solution.py:161
  42.6 2.0 constant_dynamic-slice_fusion.8
  44.6 6.1 %collective-permute-start.5 = (f32[8,8,1024]{2,1,0:T(8,128)}, f32[8,8,1024]{2,1,0:T(8,128)}, u32[]{:S(2)}, u32[]{:S(2)}) collective-permute-start(f32[8,8,1024]{2,1,0:T(8,128)} %get-tuple-element.62), channel_id=1, source_target_pairs={{0,24},{12,4},{16,8},{20,12},{24,16},{28,20},{1,25},{13,5},{17,9},... | collective-permute-start | bytes 786440 | tf_op jit(solution)/shard_map/ppermute | solution.py:244
  60.6 2.5 collective-permute-done.9
  64.4 9.1 %collective-permute-done.10 = f32[8,8,1024]{2,1,0:T(8,128)} collective-permute-done((f32[8,8,1024]{2,1,0:T(8,128)S(1)}, f32[8,8,1024]{2,1,0:T(8,128)}, u32[]{:S(2)}, u32[]{:S(2)}) %collective-permute-start.10) | collective-permute-done | bytes 262176 | tf_op jit(solution)/shard_map/ppermute | solution.py:244
  76.9 3.3 collective-permute-start.28
  80.3 5.9 %collective-permute-start.23 = (f32[8,2,8,1024]{3,2,1,0:T(8,128)S(1)}, f32[8,2,8,1024]{3,2,1,0:T(8,128)S(1)}, u32[]{:S(2)}, u32[]{:S(2)}) collective-permute-start(f32[8,2,8,1024]{3,2,1,0:T(8,128)S(1)} %get-tuple-element.93), channel_id=1, source_target_pairs={{24,28},{28,0},{25,29},{29,1},{26,30},{30,2},{27,31},{31,3}} | collective-permute-start | bytes 1572872 | tf_op jit(solution)/shard_map/ppermute | solution.py:244
  89.9 6.8 %fusion.18 = f32[8,64,512]{2,1,0:T(8,128)S(1)} fusion(s32[8,512]{1,0:T(8,128)S(1)} %bitcast.62, f32[64,8,1024]{2,1,0:T(8,128)S(1)} %select_dynamic-update-slice_fusion.8, f32[8,512]{1,0:T(8,128)S(1)} %bitcast.63), kind=kOutput, calls=%fused_computation.19 | convolution fusion | flops 3225944064 | bytes 3178496 | tf_op jit(solution)/shard_map/erl,rlo->reo/dot_general | solution.py:199
  99.2 6.8 %fusion.12 = f32[64,1,8,8,128]{4,0,3,2,1:T(8,128)S(1)} fusion(f32[64,8,8,128]{3,1,2,0:T(8,128)S(1)} %bitcast.61, s32[8,8,64]{2,1,0:T(8,128)S(1)} %get-tuple-element.142, s32[8,8,64]{2,1,0:T(8,128)S(1)} %get-tuple-element.143, s32[8,8,64]{2,1,0:T(8,128)S(1)} %get-tuple-element.141, f32[8,8,64]{2,1,0:T(8,128)S(1)} %divide_multiply_fusion), kind=kOutput, calls=%fused_computation.15 | convolution fusion | flops 405274624 | bytes 4259840 | tf_op jit(solution)/shard_map/rbek,kfrbc->efrbc/dot_general | solution.py:227
  110.3 3.5 %broadcast_in_dim.4 = f32[8,3,64,1024]{3,2,1,0:T(8,128)} broadcast(f32[]{:T(128)} %constant.109.clone.1), dimensions={} | broadcast | bytes 6291460 | tf_op jit(solution)/shard_map/broadcast_in_dim | solution.py:338
  117.2 5.5 %collective-permute-start.32 = (f32[8,2,8,1024]{3,2,1,0:T(8,128)S(1)}, f32[8,2,8,1024]{3,2,1,0:T(8,128)S(1)}, u32[]{:S(2)}, u32[]{:S(2)}) collective-permute-start(f32[8,2,8,1024]{3,2,1,0:T(8,128)S(1)} %copy-done.9), channel_id=1, source_target_pairs={{0,20},{4,24},{16,4},{20,8},{24,12},{28,16},{1,21},{5,25},{17,5},{... | collective-permute-start | bytes 1572872 | tf_op jit(solution)/shard_map/ppermute | solution.py:244
  124.2 5.0 %collective-permute-start.34 = (f32[8,2,8,1024]{3,2,1,0:T(8,128)S(1)}, f32[8,2,8,1024]{3,2,1,0:T(8,128)S(1)}, u32[]{:S(2)}, u32[]{:S(2)}) collective-permute-start(f32[8,2,8,1024]{3,2,1,0:T(8,128)S(1)} %copy-done.8), channel_id=1, source_target_pairs={{0,24},{12,4},{16,8},{20,12},{24,16},{28,20},{1,25},{13,5},{17,9},... | collective-permute-start | bytes 1572872 | tf_op jit(solution)/shard_map/ppermute | solution.py:244
  129.2 5.1 %collective-permute-done.27 = f32[8,2,8,1024]{3,2,1,0:T(8,128)S(1)} collective-permute-done((f32[8,2,8,1024]{3,2,1,0:T(8,128)S(1)}, f32[8,2,8,1024]{3,2,1,0:T(8,128)S(1)}, u32[]{:S(2)}, u32[]{:S(2)}) %collective-permute-start.27) | collective-permute-done | bytes 524320 | tf_op jit(solution)/shard_map/ppermute | solution.py:244
  135.7 28.4 %collective-permute-start.36 = (f32[8,2,8,1024]{3,2,1,0:T(8,128)S(1)}, f32[8,2,8,1024]{3,2,1,0:T(8,128)S(1)}, u32[]{:S(2)}, u32[]{:S(2)}) collective-permute-start(f32[8,2,8,1024]{3,2,1,0:T(8,128)S(1)} %copy-done.7), channel_id=1, source_target_pairs={{8,4},{12,8},{16,12},{20,16},{24,20},{28,24},{9,5},{13,9},{17,13},... | collective-permute-start | bytes 1572872 | tf_op jit(solution)/shard_map/ppermute | solution.py:244
  166.8 6.0 %collective-permute-done.31 = f32[8,2,8,1024]{3,2,1,0:T(8,128)S(1)} collective-permute-done((f32[8,2,8,1024]{3,2,1,0:T(8,128)S(1)}, f32[8,2,8,1024]{3,2,1,0:T(8,128)S(1)}, u32[]{:S(2)}, u32[]{:S(2)}) %collective-permute-start.31) | collective-permute-done | bytes 524320 | tf_op jit(solution)/shard_map/ppermute | solution.py:244
  172.8 4.7 %collective-permute-start.16 = (f32[8,1,8,1024]{3,1,2,0:T(1,128)S(1)}, f32[8,1,8,1024]{3,1,2,0:T(1,128)S(1)}, u32[]{:S(2)}, u32[]{:S(2)}) collective-permute-start(f32[8,1,8,1024]{3,1,2,0:T(1,128)S(1)} %bitcast.59), channel_id=1, source_target_pairs={{0,4},{4,8},{8,12},{12,16},{16,20},{20,24},{24,28},{28,0},{1,5},{5... | collective-permute-start | bytes 786440 | tf_op jit(solution)/shard_map/ppermute | solution.py:244
  177.6 5.0 %collective-permute-done.33 = f32[8,2,8,1024]{3,2,1,0:T(8,128)S(1)} collective-permute-done((f32[8,2,8,1024]{3,2,1,0:T(8,128)S(1)}, f32[8,2,8,1024]{3,2,1,0:T(8,128)S(1)}, u32[]{:S(2)}, u32[]{:S(2)}) %collective-permute-start.33) | collective-permute-done | bytes 524320 | tf_op jit(solution)/shard_map/ppermute | solution.py:244
  182.7 19.7 %collective-permute-start.18 = (f32[8,1,8,1024]{3,1,2,0:T(1,128)}, f32[8,1,8,1024]{3,1,2,0:T(1,128)}, u32[]{:S(2)}, u32[]{:S(2)}) collective-permute-start(f32[8,1,8,1024]{3,1,2,0:T(1,128)} %bitcast.15), channel_id=1, source_target_pairs={{0,12},{4,16},{8,20},{12,24},{16,28},{20,0},{24,4},{28,8},{1,13},{... | collective-permute-start | bytes 786440 | tf_op jit(solution)/shard_map/ppermute | solution.py:244
  205.1 9.1 %fusion.5 = f32[64,2,8,8,128]{4,0,1,3,2:T(8,128)S(1)} fusion(f32[64,2,8,8,128]{4,2,3,1,0:T(8,128)S(1)} %bitcast.60, s32[8,8,64]{2,1,0:T(8,128)S(1)} %get-tuple-element.142, s32[8,8,64]{2,1,0:T(8,128)S(1)} %get-tuple-element.143, s32[8,8,64]{2,1,0:T(8,128)S(1)} %get-tuple-element.141, f32[8,8,64]{2,1,0:T(8,128)S(1)} %divide_multiply_fusion), kind=kOutput, calls=%fused_computation.6 | convolution fusion | flops 807927808 | bytes 8454144 | tf_op jit(solution)/shard_map/rbek,kfrbc->efrbc/dot_general | solution.py:227
  216.4 4.3 %collective-permute-start.22 = (f32[8,1,8,1024]{3,1,2,0:T(1,128)}, f32[8,1,8,1024]{3,1,2,0:T(1,128)}, u32[]{:S(2)}, u32[]{:S(2)}) collective-permute-start(f32[8,1,8,1024]{3,1,2,0:T(1,128)} %bitcast.19), channel_id=1, source_target_pairs={{0,28},{4,0},{8,4},{12,8},{16,12},{20,16},{24,20},{28,24},{1,29},{... | collective-permute-start | bytes 786440 | tf_op jit(solution)/shard_map/ppermute | solution.py:244
  226.9 2.0 copy.32
  237.0 6.6 %collective-permute-done.20 = f32[8,1,8,1024]{3,1,2,0:T(1,128)S(1)} collective-permute-done((f32[8,1,8,1024]{3,1,2,0:T(1,128)}, f32[8,1,8,1024]{3,1,2,0:T(1,128)S(1)}, u32[]{:S(2)}, u32[]{:S(2)}) %collective-permute-start.20) | collective-permute-done | bytes 262176 | tf_op jit(solution)/shard_map/ppermute | solution.py:244
  243.6 14.1 %collective-permute-start.39 = (f32[8,2,8,1024]{3,2,1,0:T(8,128)}, f32[8,2,8,1024]{3,2,1,0:T(8,128)}, u32[]{:S(2)}, u32[]{:S(2)}) collective-permute-start(f32[8,2,8,1024]{3,2,1,0:T(8,128)} %slice.139), channel_id=1, source_target_pairs={{0,12},{4,16},{8,20},{12,24},{16,28},{20,0},{24,4},{28,8},{1,13},{... | collective-permute-start | bytes 1572872 | tf_op jit(solution)/shard_map/ppermute | solution.py:244
  259.6 14.2 %collective-permute-start.40 = (f32[8,2,8,1024]{3,2,1,0:T(8,128)}, f32[8,2,8,1024]{3,2,1,0:T(8,128)}, u32[]{:S(2)}, u32[]{:S(2)}) collective-permute-start(f32[8,2,8,1024]{3,2,1,0:T(8,128)} %slice.141), channel_id=1, source_target_pairs={{0,16},{4,20},{8,24},{12,28},{16,0},{20,4},{24,8},{28,12},{1,17},{... | collective-permute-start | bytes 1572872 | tf_op jit(solution)/shard_map/ppermute | solution.py:244
  281.2 2.4 collective-permute-start.43
  287.4 32.5 %collective-permute-done.40 = f32[8,2,8,1024]{3,2,1,0:T(8,128)} collective-permute-done((f32[8,2,8,1024]{3,2,1,0:T(8,128)}, f32[8,2,8,1024]{3,2,1,0:T(8,128)}, u32[]{:S(2)}, u32[]{:S(2)}) %collective-permute-start.40) | collective-permute-done | bytes 524320 | tf_op jit(solution)/shard_map/ppermute | solution.py:244
  321.8 16.5 %collective-permute-done.41 = f32[8,2,8,1024]{3,2,1,0:T(8,128)S(1)} collective-permute-done((f32[8,2,8,1024]{3,2,1,0:T(8,128)S(1)}, f32[8,2,8,1024]{3,2,1,0:T(8,128)S(1)}, u32[]{:S(2)}, u32[]{:S(2)}) %collective-permute-start.41) | collective-permute-done | bytes 524320 | tf_op jit(solution)/shard_map/ppermute | solution.py:244
  (166 shorter events, 79.2 us)
Async XLA Ops:
  11.2 33.4 %collective-permute-start = (f32[8,8,1024]{2,1,0:T(8,128)}, f32[8,8,1024]{2,1,0:T(8,128)S(1)}, u32[]{:S(2)}, u32[]{:S(2)}) collective-permute-start(f32[8,8,1024]{2,1,0:T(8,128)} %get-tuple-element.57), channel_id=1, source_target_pairs={{0,4},{4,8},{8,12},{12,16},{16,20},{20,24},{1,5},{5,9},{9,13},{13,... | collective-permute-start | bytes 786440 | tf_op jit(solution)/shard_map/ppermute | solution.py:244
  11.9 38.8 %collective-permute-start.1 = (f32[8,8,1024]{2,1,0:T(8,128)}, f32[8,8,1024]{2,1,0:T(8,128)}, u32[]{:S(2)}, u32[]{:S(2)}) collective-permute-start(f32[8,8,1024]{2,1,0:T(8,128)} %get-tuple-element.58), channel_id=1, source_target_pairs={{0,8},{4,12},{8,16},{12,20},{16,24},{28,4},{1,9},{5,13},{9,17},{13... | collective-permute-start | bytes 786440 | tf_op jit(solution)/shard_map/ppermute | solution.py:244
  17.5 35.2 %collective-permute-start.2 = (f32[8,8,1024]{2,1,0:T(8,128)}, f32[8,8,1024]{2,1,0:T(8,128)}, u32[]{:S(2)}, u32[]{:S(2)}) collective-permute-start(f32[8,8,1024]{2,1,0:T(8,128)} %get-tuple-element.59), channel_id=1, source_target_pairs={{0,12},{4,16},{8,20},{12,24},{24,4},{28,8},{1,13},{5,17},{9,21},{1... | collective-permute-start | bytes 786440 | tf_op jit(solution)/shard_map/ppermute | solution.py:244
  28.9 25.8 %collective-permute-start.3 = (f32[8,8,1024]{2,1,0:T(8,128)}, f32[8,8,1024]{2,1,0:T(8,128)}, u32[]{:S(2)}, u32[]{:S(2)}) collective-permute-start(f32[8,8,1024]{2,1,0:T(8,128)} %get-tuple-element.60), channel_id=1, source_target_pairs={{0,16},{4,20},{8,24},{20,4},{24,8},{28,12},{1,17},{5,21},{9,25},{2... | collective-permute-start | bytes 786440 | tf_op jit(solution)/shard_map/ppermute | solution.py:244
  31.5 25.0 %collective-permute-start.4 = (f32[8,8,1024]{2,1,0:T(8,128)}, f32[8,8,1024]{2,1,0:T(8,128)}, u32[]{:S(2)}, u32[]{:S(2)}) collective-permute-start(f32[8,8,1024]{2,1,0:T(8,128)} %get-tuple-element.61), channel_id=1, source_target_pairs={{0,20},{4,24},{16,4},{20,8},{24,12},{28,16},{1,21},{5,25},{17,5},{... | collective-permute-start | bytes 786440 | tf_op jit(solution)/shard_map/ppermute | solution.py:244
  54.7 18.8 %collective-permute-start.10 = (f32[8,8,1024]{2,1,0:T(8,128)S(1)}, f32[8,8,1024]{2,1,0:T(8,128)}, u32[]{:S(2)}, u32[]{:S(2)}) collective-permute-start(f32[8,8,1024]{2,1,0:T(8,128)S(1)} %get-tuple-element.68), channel_id=1, source_target_pairs={{20,28},{24,0},{21,29},{25,1},{22,30},{26,2},{23,31},{27,3}} | collective-permute-start | bytes 786440 | tf_op jit(solution)/shard_map/ppermute | solution.py:244
  74.9 39.7 %collective-permute-start.24 = (f32[8,2,8,1024]{3,2,1,0:T(8,128)S(1)}, f32[8,2,8,1024]{3,2,1,0:T(8,128)S(1)}, u32[]{:S(2)}, u32[]{:S(2)}) collective-permute-start(f32[8,2,8,1024]{3,2,1,0:T(8,128)S(1)} %copy-done.13), channel_id=1, source_target_pairs={{0,4},{4,8},{8,12},{12,16},{16,20},{20,24},{1,5},{5,9},{9,13},{13,... | collective-permute-start | bytes 1572872 | tf_op jit(solution)/shard_map/ppermute | solution.py:244
  75.6 41.6 %collective-permute-start.26 = (f32[8,2,8,1024]{3,2,1,0:T(8,128)S(1)}, f32[8,2,8,1024]{3,2,1,0:T(8,128)S(1)}, u32[]{:S(2)}, u32[]{:S(2)}) collective-permute-start(f32[8,2,8,1024]{3,2,1,0:T(8,128)S(1)} %copy-done.12), channel_id=1, source_target_pairs={{0,8},{4,12},{8,16},{12,20},{16,24},{28,4},{1,9},{5,13},{9,17},{13... | collective-permute-start | bytes 1572872 | tf_op jit(solution)/shard_map/ppermute | solution.py:244
  76.9 47.2 %collective-permute-start.28 = (f32[8,2,8,1024]{3,2,1,0:T(8,128)S(1)}, f32[8,2,8,1024]{3,2,1,0:T(8,128)S(1)}, u32[]{:S(2)}, u32[]{:S(2)}) collective-permute-start(f32[8,2,8,1024]{3,2,1,0:T(8,128)S(1)} %copy-done.11), channel_id=1, source_target_pairs={{0,12},{4,16},{8,20},{12,24},{24,4},{28,8},{1,13},{5,17},{9,21},{1... | collective-permute-start | bytes 1572872 | tf_op jit(solution)/shard_map/ppermute | solution.py:244
  80.3 35.5 %collective-permute-start.23 = (f32[8,2,8,1024]{3,2,1,0:T(8,128)S(1)}, f32[8,2,8,1024]{3,2,1,0:T(8,128)S(1)}, u32[]{:S(2)}, u32[]{:S(2)}) collective-permute-start(f32[8,2,8,1024]{3,2,1,0:T(8,128)S(1)} %get-tuple-element.93), channel_id=1, source_target_pairs={{24,28},{28,0},{25,29},{29,1},{26,30},{30,2},{27,31},{31,3}} | collective-permute-start | bytes 1572872 | tf_op jit(solution)/shard_map/ppermute | solution.py:244
  86.2 36.6 %collective-permute-start.25 = (f32[8,2,8,1024]{3,2,1,0:T(8,128)S(1)}, f32[8,2,8,1024]{3,2,1,0:T(8,128)S(1)}, u32[]{:S(2)}, u32[]{:S(2)}) collective-permute-start(f32[8,2,8,1024]{3,2,1,0:T(8,128)S(1)} %get-tuple-element.95), channel_id=1, source_target_pairs={{20,28},{24,0},{21,29},{25,1},{22,30},{26,2},{23,31},{27,3}} | collective-permute-start | bytes 1572872 | tf_op jit(solution)/shard_map/ppermute | solution.py:244
  114.5 21.2 %collective-permute-start.30 = (f32[8,2,8,1024]{3,2,1,0:T(8,128)S(1)}, f32[8,2,8,1024]{3,2,1,0:T(8,128)S(1)}, u32[]{:S(2)}, u32[]{:S(2)}) collective-permute-start(f32[8,2,8,1024]{3,2,1,0:T(8,128)S(1)} %copy-done.10), channel_id=1, source_target_pairs={{0,16},{4,20},{8,24},{20,4},{24,8},{28,12},{1,17},{5,21},{9,25},{2... | collective-permute-start | bytes 1572872 | tf_op jit(solution)/shard_map/ppermute | solution.py:244
  117.2 48.2 %collective-permute-start.32 = (f32[8,2,8,1024]{3,2,1,0:T(8,128)S(1)}, f32[8,2,8,1024]{3,2,1,0:T(8,128)S(1)}, u32[]{:S(2)}, u32[]{:S(2)}) collective-permute-start(f32[8,2,8,1024]{3,2,1,0:T(8,128)S(1)} %copy-done.9), channel_id=1, source_target_pairs={{0,20},{4,24},{16,4},{20,8},{24,12},{28,16},{1,21},{5,25},{17,5},{... | collective-permute-start | bytes 1572872 | tf_op jit(solution)/shard_map/ppermute | solution.py:244
  122.8 41.3 %collective-permute-start.29 = (f32[8,2,8,1024]{3,2,1,0:T(8,128)S(1)}, f32[8,2,8,1024]{3,2,1,0:T(8,128)S(1)}, u32[]{:S(2)}, u32[]{:S(2)}) collective-permute-start(f32[8,2,8,1024]{3,2,1,0:T(8,128)S(1)} %get-tuple-element.99), channel_id=1, source_target_pairs={{12,28},{16,0},{13,29},{17,1},{14,30},{18,2},{15,31},{19,3}} | collective-permute-start | bytes 1572872 | tf_op jit(solution)/shard_map/ppermute | solution.py:244
  124.2 53.4 %collective-permute-start.34 = (f32[8,2,8,1024]{3,2,1,0:T(8,128)S(1)}, f32[8,2,8,1024]{3,2,1,0:T(8,128)S(1)}, u32[]{:S(2)}, u32[]{:S(2)}) collective-permute-start(f32[8,2,8,1024]{3,2,1,0:T(8,128)S(1)} %copy-done.8), channel_id=1, source_target_pairs={{0,24},{12,4},{16,8},{20,12},{24,16},{28,20},{1,25},{13,5},{17,9},... | collective-permute-start | bytes 1572872 | tf_op jit(solution)/shard_map/ppermute | solution.py:244
  134.3 38.5 %collective-permute-start.31 = (f32[8,2,8,1024]{3,2,1,0:T(8,128)S(1)}, f32[8,2,8,1024]{3,2,1,0:T(8,128)S(1)}, u32[]{:S(2)}, u32[]{:S(2)}) collective-permute-start(f32[8,2,8,1024]{3,2,1,0:T(8,128)S(1)} %get-tuple-element.101), channel_id=1, source_target_pairs={{8,28},{12,0},{9,29},{13,1},{10,30},{14,2},{11,31},{15,3}} | collective-permute-start | bytes 1572872 | tf_op jit(solution)/shard_map/ppermute | solution.py:244
  135.7 66.8 %collective-permute-start.36 = (f32[8,2,8,1024]{3,2,1,0:T(8,128)S(1)}, f32[8,2,8,1024]{3,2,1,0:T(8,128)S(1)}, u32[]{:S(2)}, u32[]{:S(2)}) collective-permute-start(f32[8,2,8,1024]{3,2,1,0:T(8,128)S(1)} %copy-done.7), channel_id=1, source_target_pairs={{8,4},{12,8},{16,12},{20,16},{24,20},{28,24},{9,5},{13,9},{17,13},... | collective-permute-start | bytes 1572872 | tf_op jit(solution)/shard_map/ppermute | solution.py:244
  165.5 37.8 %collective-permute-start.35 = (f32[8,2,8,1024]{3,2,1,0:T(8,128)S(1)}, f32[8,2,8,1024]{3,2,1,0:T(8,128)S(1)}, u32[]{:S(2)}, u32[]{:S(2)}) collective-permute-start(f32[8,2,8,1024]{3,2,1,0:T(8,128)S(1)} %get-tuple-element.105), channel_id=1, source_target_pairs={{0,28},{4,0},{1,29},{5,1},{2,30},{6,2},{3,31},{7,3}} | collective-permute-start | bytes 1572872 | tf_op jit(solution)/shard_map/ppermute | solution.py:244
  172.8 42.7 %collective-permute-start.16 = (f32[8,1,8,1024]{3,1,2,0:T(1,128)S(1)}, f32[8,1,8,1024]{3,1,2,0:T(1,128)S(1)}, u32[]{:S(2)}, u32[]{:S(2)}) collective-permute-start(f32[8,1,8,1024]{3,1,2,0:T(1,128)S(1)} %bitcast.59), channel_id=1, source_target_pairs={{0,4},{4,8},{8,12},{12,16},{16,20},{20,24},{24,28},{28,0},{1,5},{5... | collective-permute-start | bytes 786440 | tf_op jit(solution)/shard_map/ppermute | solution.py:244
  177.6 38.8 %collective-permute-start.17 = (f32[8,1,8,1024]{3,1,2,0:T(1,128)S(1)}, f32[8,1,8,1024]{3,1,2,0:T(1,128)S(1)}, u32[]{:S(2)}, u32[]{:S(2)}) collective-permute-start(f32[8,1,8,1024]{3,1,2,0:T(1,128)S(1)} %bitcast.58), channel_id=1, source_target_pairs={{0,8},{4,12},{8,16},{12,20},{16,24},{20,28},{24,0},{28,4},{1,9},{5... | collective-permute-start | bytes 786440 | tf_op jit(solution)/shard_map/ppermute | solution.py:244
  182.7 41.7 %collective-permute-start.18 = (f32[8,1,8,1024]{3,1,2,0:T(1,128)}, f32[8,1,8,1024]{3,1,2,0:T(1,128)}, u32[]{:S(2)}, u32[]{:S(2)}) collective-permute-start(f32[8,1,8,1024]{3,1,2,0:T(1,128)} %bitcast.15), channel_id=1, source_target_pairs={{0,12},{4,16},{8,20},{12,24},{16,28},{20,0},{24,4},{28,8},{1,13},{... | collective-permute-start | bytes 786440 | tf_op jit(solution)/shard_map/ppermute | solution.py:244
  202.5 28.4 %collective-permute-start.19 = (f32[8,1,8,1024]{3,1,2,0:T(1,128)}, f32[8,1,8,1024]{3,1,2,0:T(1,128)}, u32[]{:S(2)}, u32[]{:S(2)}) collective-permute-start(f32[8,1,8,1024]{3,1,2,0:T(1,128)} %bitcast.16), channel_id=1, source_target_pairs={{0,16},{4,20},{8,24},{12,28},{16,0},{20,4},{24,8},{28,12},{1,17},{... | collective-permute-start | bytes 786440 | tf_op jit(solution)/shard_map/ppermute | solution.py:244
  203.3 40.3 %collective-permute-start.20 = (f32[8,1,8,1024]{3,1,2,0:T(1,128)}, f32[8,1,8,1024]{3,1,2,0:T(1,128)S(1)}, u32[]{:S(2)}, u32[]{:S(2)}) collective-permute-start(f32[8,1,8,1024]{3,1,2,0:T(1,128)} %bitcast.17), channel_id=1, source_target_pairs={{0,20},{4,24},{8,28},{12,0},{16,4},{20,8},{24,12},{28,16},{1,21},{... | collective-permute-start | bytes 786440 | tf_op jit(solution)/shard_map/ppermute | solution.py:244
  215.6 44.0 %collective-permute-start.21 = (f32[8,1,8,1024]{3,1,2,0:T(1,128)}, f32[8,1,8,1024]{3,1,2,0:T(1,128)}, u32[]{:S(2)}, u32[]{:S(2)}) collective-permute-start(f32[8,1,8,1024]{3,1,2,0:T(1,128)} %bitcast.18), channel_id=1, source_target_pairs={{0,24},{4,28},{8,0},{12,4},{16,8},{20,12},{24,16},{28,20},{1,25},{... | collective-permute-start | bytes 786440 | tf_op jit(solution)/shard_map/ppermute | solution.py:244
  216.4 59.6 %collective-permute-start.22 = (f32[8,1,8,1024]{3,1,2,0:T(1,128)}, f32[8,1,8,1024]{3,1,2,0:T(1,128)}, u32[]{:S(2)}, u32[]{:S(2)}) collective-permute-start(f32[8,1,8,1024]{3,1,2,0:T(1,128)} %bitcast.19), channel_id=1, source_target_pairs={{0,28},{4,0},{8,4},{12,8},{16,12},{20,16},{24,20},{28,24},{1,29},{... | collective-permute-start | bytes 786440 | tf_op jit(solution)/shard_map/ppermute | solution.py:244
  224.4 54.8 %collective-permute-start.37 = (f32[8,2,8,1024]{3,2,1,0:T(8,128)}, f32[8,2,8,1024]{3,2,1,0:T(8,128)}, u32[]{:S(2)}, u32[]{:S(2)}) collective-permute-start(f32[8,2,8,1024]{3,2,1,0:T(8,128)} %slice.135), channel_id=1, source_target_pairs={{0,4},{4,8},{8,12},{12,16},{16,20},{20,24},{24,28},{28,0},{1,5},{5... | collective-permute-start | bytes 1572872 | tf_op jit(solution)/shard_map/ppermute | solution.py:244
  230.8 50.3 %collective-permute-start.38 = (f32[8,2,8,1024]{3,2,1,0:T(8,128)}, f32[8,2,8,1024]{3,2,1,0:T(8,128)}, u32[]{:S(2)}, u32[]{:S(2)}) collective-permute-start(f32[8,2,8,1024]{3,2,1,0:T(8,128)} %slice.137), channel_id=1, source_target_pairs={{0,8},{4,12},{8,16},{12,20},{16,24},{20,28},{24,0},{28,4},{1,9},{5... | collective-permute-start | bytes 1572872 | tf_op jit(solution)/shard_map/ppermute | solution.py:244
  243.6 41.9 %collective-permute-start.39 = (f32[8,2,8,1024]{3,2,1,0:T(8,128)}, f32[8,2,8,1024]{3,2,1,0:T(8,128)}, u32[]{:S(2)}, u32[]{:S(2)}) collective-permute-start(f32[8,2,8,1024]{3,2,1,0:T(8,128)} %slice.139), channel_id=1, source_target_pairs={{0,12},{4,16},{8,20},{12,24},{16,28},{20,0},{24,4},{28,8},{1,13},{... | collective-permute-start | bytes 1572872 | tf_op jit(solution)/shard_map/ppermute | solution.py:244
  259.6 60.3 %collective-permute-start.40 = (f32[8,2,8,1024]{3,2,1,0:T(8,128)}, f32[8,2,8,1024]{3,2,1,0:T(8,128)}, u32[]{:S(2)}, u32[]{:S(2)}) collective-permute-start(f32[8,2,8,1024]{3,2,1,0:T(8,128)} %slice.141), channel_id=1, source_target_pairs={{0,16},{4,20},{8,24},{12,28},{16,0},{20,4},{24,8},{28,12},{1,17},{... | collective-permute-start | bytes 1572872 | tf_op jit(solution)/shard_map/ppermute | solution.py:244
  276.0 62.3 %collective-permute-start.41 = (f32[8,2,8,1024]{3,2,1,0:T(8,128)S(1)}, f32[8,2,8,1024]{3,2,1,0:T(8,128)S(1)}, u32[]{:S(2)}, u32[]{:S(2)}) collective-permute-start(f32[8,2,8,1024]{3,2,1,0:T(8,128)S(1)} %slice.143), channel_id=1, source_target_pairs={{0,20},{4,24},{8,28},{12,0},{16,4},{20,8},{24,12},{28,16},{1,21},{... | collective-permute-start | bytes 1572872 | tf_op jit(solution)/shard_map/ppermute | solution.py:244
  279.2 59.9 %collective-permute-start.42 = (f32[8,2,8,1024]{3,2,1,0:T(8,128)S(1)}, f32[8,2,8,1024]{3,2,1,0:T(8,128)S(1)}, u32[]{:S(2)}, u32[]{:S(2)}) collective-permute-start(f32[8,2,8,1024]{3,2,1,0:T(8,128)S(1)} %slice.145), channel_id=1, source_target_pairs={{0,24},{4,28},{8,0},{12,4},{16,8},{20,12},{24,16},{28,20},{1,25},{... | collective-permute-start | bytes 1572872 | tf_op jit(solution)/shard_map/ppermute | solution.py:244
  281.2 58.8 %collective-permute-start.43 = (f32[8,2,8,1024]{3,2,1,0:T(8,128)S(1)}, f32[8,2,8,1024]{3,2,1,0:T(8,128)S(1)}, u32[]{:S(2)}, u32[]{:S(2)}) collective-permute-start(f32[8,2,8,1024]{3,2,1,0:T(8,128)S(1)} %slice.147), channel_id=1, source_target_pairs={{0,28},{4,0},{8,4},{12,8},{16,12},{20,16},{24,20},{28,24},{1,29},{... | collective-permute-start | bytes 1572872 | tf_op jit(solution)/shard_map/ppermute | solution.py:244
  (27 other events, 430.4 us)

commit v3 on v2

--- a/solution.py
+++ b/solution.py
@@ -303,15 +303,12 @@
     outer = [j for j in range(count) if j not in inner]
     factors = coriolis_frame(coriolis, band_index, count_of_rows)
 
+    before, after = edge_rows(particle_states, "dom", 2, margin)
     heights, winds = early_pieces(particle_states, factors, "mem")
     inner_heights = send_all(heights, "mem", inner)
-    states, heights = lax.optimization_barrier((particle_states, heights))
-    before, after = edge_rows(states, "dom", 2, margin)
+    edges = edge_forecast(particle_states, before, after, factors, band_index, lax.axis_size("dom"))
+    outer_heights = send_all(edge_pieces(edges[0], "mem", 1, piece), "mem", outer)
     inner_winds = send_all(winds, "mem", inner)
-    edges = edge_forecast(
-        states, before, after, factors, band_index, lax.axis_size("dom")
-    )
-    outer_heights = send_all(edge_pieces(edges[0], "mem", 1, piece), "mem", outer)
     outer_winds = send_all(edge_pieces(edges[1], "mem", 2, piece), "mem", outer)
     inner_heights, outer_heights = lax.optimization_barrier((inner_heights, outer_heights))
     is_outer = jnp.any(jnp.stack([own == j for j in outer]))

time: 343 us -> 347 us (1.012)
  transfers between devices with their start and end apart: 44 -> 44, of which waited for: 8 -> 9; matrix products, arithmetic and copies ran while one was open for 22% -> 22% of each run, Pallas kernels for 3% -> 5%
where the time goes in v3:
time: 347 us; the launch traced here: 345 us
  starting transfers between devices  161 us (46%)
  waiting for transfers between devices  86.8 us (25%)
  local copies, waits for them, and re-layouts  47.6 us (14%)
  matrix products  23.7 us (7%)
  Pallas kernels  18.8 us (5%)
  other arithmetic  5.95 us (2%)
    ppermute x42, starting transfers between devices, send_all(): received[d] = lax.ppermute(pieces[d], axis, shifts(count, d, targets))  157 us
    ppermute x42, waiting for transfers between devices, send_all(): received[d] = lax.ppermute(pieces[d], axis, shifts(count, d, targets))  86.8 us
    dynamic_update_slice x16, local copies, waits for them, and re-layouts, put_back(): whole = lax.dynamic_update_slice(whole, piece, (0, field, start, 0))  20.7 us
    slice x26, local copies, waits for them, and re-layouts, hand_back(): updated[d * members_dev:(d + 1) * members_dev]  17.4 us
    dot_general x2, matrix products, merge_fields(): jnp.einsum('rbek,kfrbc->efrbc', mixing, blocks, precision=lax.Precision.H...  15.9 us
    pallas_call x1, Pallas kernels, early_pieces(): pl.pallas_call(functools.partial(early_kernel, count), grid=(members,), i...  9.75 us
    pallas_call x1, Pallas kernels, edge_forecast(): pl.pallas_call(edge_kernel, grid=(members,), in_specs=[pl.BlockSpec(memor...  9.02 us
  transfers between devices with their start and end apart: 44, of which 9 were waited for; matrix products, arithmetic and copies ran while one was open for 22% of the time, Pallas kernels for 5%

profile of v3, /device:TPU:28, one launch (start us, length us, event | category | flops | bytes accessed | tf_op | source)
XLA Modules:
  0.0 345.3 jit_solution(1602668015622862259)
XLA Ops:
  2.9 3.1 collective-permute-start.7
  7.4 9.7 %shard_map.55 = (f32[8,8,1024]{2,1,0:T(8,128)}, f32[8,8,1024]{2,1,0:T(8,128)}, f32[8,8,1024]{2,1,0:T(8,128)}, f32[8,8,1024]{2,1,0:T(8,128)}, f32[8,8,1024]{2,1,0...) custom-call(s32[1]{0:T(128)} %bitcast.place_ref, ...), custom_call_target="tpu_custom_call" | custom-call | flops 125829120 | bytes 12582912 | tf_op jit(solution)/shard_map/pallas_call | solution.py:136
  17.8 5.6 %collective-permute-start.1 = (f32[8,8,1024]{2,1,0:T(8,128)}, f32[8,8,1024]{2,1,0:T(8,128)}, u32[]{:S(2)}, u32[]{:S(2)}) collective-permute-start(f32[8,8,1024]{2,1,0:T(8,128)} %get-tuple-element.57), channel_id=1, source_target_pairs={{0,8},{4,12},{8,16},{12,20},{16,24},{28,4},{1,9},{5,13},{9,17},{13... | collective-permute-start | bytes 786440 | tf_op jit(solution)/shard_map/ppermute | solution.py:244
  23.4 3.5 %collective-permute-start.2 = (f32[8,8,1024]{2,1,0:T(8,128)}, f32[8,8,1024]{2,1,0:T(8,128)}, u32[]{:S(2)}, u32[]{:S(2)}) collective-permute-start(f32[8,8,1024]{2,1,0:T(8,128)} %get-tuple-element.58), channel_id=1, source_target_pairs={{0,12},{4,16},{8,20},{12,24},{24,4},{28,8},{1,13},{5,17},{9,21},{1... | collective-permute-start | bytes 786440 | tf_op jit(solution)/shard_map/ppermute | solution.py:244
  28.9 2.0 collective-permute-start.3
  33.6 9.0 %shard_map.56 = (f32[8,16,1024]{2,1,0:T(8,128)}, f32[8,2,16,1024]{3,2,1,0:T(8,128)}) custom-call(f32[2]{0:T(128)} %add_convert_fusion.inside_ref, f32[96,128]{1,0:T(8,128)} %broadcast_in_dim.5.coriolis_ref, f32[8,3,64,1024]{3,2,1,0:T(8,128)} %high_ref.1, f32[8,3,64,1024]{3,2,1,0:T(8,128)} %high_ref.1, f32[8,3,4,1024]{3,2,1,0:T(4,128)} %copy-done.3, ...), custom_call_target="tpu_custom_call" | custom-call | flops 94371840 | bytes 9437184 | tf_op jit(solution)/shard_map/pallas_call | solution.py:161
  42.6 2.0 constant_dynamic-slice_fusion.8
  44.6 6.1 %collective-permute-start.5 = (f32[8,8,1024]{2,1,0:T(8,128)}, f32[8,8,1024]{2,1,0:T(8,128)}, u32[]{:S(2)}, u32[]{:S(2)}) collective-permute-start(f32[8,8,1024]{2,1,0:T(8,128)} %get-tuple-element.61), channel_id=1, source_target_pairs={{0,24},{12,4},{16,8},{20,12},{24,16},{28,20},{1,25},{13,5},{17,9},... | collective-permute-start | bytes 786440 | tf_op jit(solution)/shard_map/ppermute | solution.py:244
  50.8 2.0 collective-permute-start.6
  62.3 14.7 %collective-permute-done.9 = f32[8,8,1024]{2,1,0:T(8,128)} collective-permute-done((f32[8,8,1024]{2,1,0:T(8,128)S(1)}, f32[8,8,1024]{2,1,0:T(8,128)}, u32[]{:S(2)}, u32[]{:S(2)}) %collective-permute-start.9) | collective-permute-done | bytes 262176 | tf_op jit(solution)/shard_map/ppermute | solution.py:244
  80.4 7.6 %collective-permute-start.26 = (f32[8,2,8,1024]{3,2,1,0:T(8,128)S(1)}, f32[8,2,8,1024]{3,2,1,0:T(8,128)S(1)}, u32[]{:S(2)}, u32[]{:S(2)}) collective-permute-start(f32[8,2,8,1024]{3,2,1,0:T(8,128)S(1)} %copy-done.12), channel_id=1, source_target_pairs={{0,8},{4,12},{8,16},{12,20},{16,24},{28,4},{1,9},{5,13},{9,17},{13... | collective-permute-start | bytes 1572872 | tf_op jit(solution)/shard_map/ppermute | solution.py:244
  89.9 2.3 collective-permute-start.23
  96.0 6.8 %fusion.18 = f32[8,64,512]{2,1,0:T(8,128)S(1)} fusion(s32[8,512]{1,0:T(8,128)S(1)} %bitcast.62, f32[64,8,1024]{2,1,0:T(8,128)S(1)} %select_dynamic-update-slice_fusion.8, f32[8,512]{1,0:T(8,128)S(1)} %bitcast.63), kind=kOutput, calls=%fused_computation.19 | convolution fusion | flops 3225944064 | bytes 3178496 | tf_op jit(solution)/shard_map/erl,rlo->reo/dot_general | solution.py:199
  105.2 6.8 %fusion.12 = f32[64,1,8,8,128]{4,0,3,2,1:T(8,128)S(1)} fusion(f32[64,8,8,128]{3,1,2,0:T(8,128)S(1)} %bitcast.61, s32[8,8,64]{2,1,0:T(8,128)S(1)} %get-tuple-element.140, s32[8,8,64]{2,1,0:T(8,128)S(1)} %get-tuple-element.141, s32[8,8,64]{2,1,0:T(8,128)S(1)} %get-tuple-element.139, f32[8,8,64]{2,1,0:T(8,128)S(1)} %divide_multiply_fusion), kind=kOutput, calls=%fused_computation.15 | convolution fusion | flops 405274624 | bytes 4259840 | tf_op jit(solution)/shard_map/rbek,kfrbc->efrbc/dot_general | solution.py:227
  116.3 3.5 %broadcast_in_dim.4 = f32[8,3,64,1024]{3,2,1,0:T(8,128)} broadcast(f32[]{:T(128)} %constant.109.clone.1), dimensions={} | broadcast | bytes 6291460 | tf_op jit(solution)/shard_map/broadcast_in_dim | solution.py:335
  123.3 5.5 %collective-permute-start.32 = (f32[8,2,8,1024]{3,2,1,0:T(8,128)S(1)}, f32[8,2,8,1024]{3,2,1,0:T(8,128)S(1)}, u32[]{:S(2)}, u32[]{:S(2)}) collective-permute-start(f32[8,2,8,1024]{3,2,1,0:T(8,128)S(1)} %copy-done.9), channel_id=1, source_target_pairs={{0,20},{4,24},{16,4},{20,8},{24,12},{28,16},{1,21},{5,25},{17,5},{... | collective-permute-start | bytes 1572872 | tf_op jit(solution)/shard_map/ppermute | solution.py:244
  130.2 6.1 %collective-permute-start.34 = (f32[8,2,8,1024]{3,2,1,0:T(8,128)S(1)}, f32[8,2,8,1024]{3,2,1,0:T(8,128)S(1)}, u32[]{:S(2)}, u32[]{:S(2)}) collective-permute-start(f32[8,2,8,1024]{3,2,1,0:T(8,128)S(1)} %copy-done.8), channel_id=1, source_target_pairs={{0,24},{12,4},{16,8},{20,12},{24,16},{28,20},{1,25},{13,5},{17,9},... | collective-permute-start | bytes 1572872 | tf_op jit(solution)/shard_map/ppermute | solution.py:244
  136.3 3.1 collective-permute-done.27
  140.8 27.7 %collective-permute-start.36 = (f32[8,2,8,1024]{3,2,1,0:T(8,128)S(1)}, f32[8,2,8,1024]{3,2,1,0:T(8,128)S(1)}, u32[]{:S(2)}, u32[]{:S(2)}) collective-permute-start(f32[8,2,8,1024]{3,2,1,0:T(8,128)S(1)} %copy-done.7), channel_id=1, source_target_pairs={{8,4},{12,8},{16,12},{20,16},{24,20},{28,24},{9,5},{13,9},{17,13},... | collective-permute-start | bytes 1572872 | tf_op jit(solution)/shard_map/ppermute | solution.py:244
  171.2 6.0 %collective-permute-done.31 = f32[8,2,8,1024]{3,2,1,0:T(8,128)S(1)} collective-permute-done((f32[8,2,8,1024]{3,2,1,0:T(8,128)S(1)}, f32[8,2,8,1024]{3,2,1,0:T(8,128)S(1)}, u32[]{:S(2)}, u32[]{:S(2)}) %collective-permute-start.31) | collective-permute-done | bytes 524320 | tf_op jit(solution)/shard_map/ppermute | solution.py:244
  177.2 4.7 %collective-permute-start.16 = (f32[8,1,8,1024]{3,1,2,0:T(1,128)S(1)}, f32[8,1,8,1024]{3,1,2,0:T(1,128)S(1)}, u32[]{:S(2)}, u32[]{:S(2)}) collective-permute-start(f32[8,1,8,1024]{3,1,2,0:T(1,128)S(1)} %bitcast.59), channel_id=1, source_target_pairs={{0,4},{4,8},{8,12},{12,16},{16,20},{20,24},{24,28},{28,0},{1,5},{5... | collective-permute-start | bytes 786440 | tf_op jit(solution)/shard_map/ppermute | solution.py:244
  182.0 5.1 %collective-permute-done.33 = f32[8,2,8,1024]{3,2,1,0:T(8,128)S(1)} collective-permute-done((f32[8,2,8,1024]{3,2,1,0:T(8,128)S(1)}, f32[8,2,8,1024]{3,2,1,0:T(8,128)S(1)}, u32[]{:S(2)}, u32[]{:S(2)}) %collective-permute-start.33) | collective-permute-done | bytes 524320 | tf_op jit(solution)/shard_map/ppermute | solution.py:244
  187.1 19.8 %collective-permute-start.18 = (f32[8,1,8,1024]{3,1,2,0:T(1,128)}, f32[8,1,8,1024]{3,1,2,0:T(1,128)}, u32[]{:S(2)}, u32[]{:S(2)}) collective-permute-start(f32[8,1,8,1024]{3,1,2,0:T(1,128)} %bitcast.15), channel_id=1, source_target_pairs={{0,12},{4,16},{8,20},{12,24},{16,28},{20,0},{24,4},{28,8},{1,13},{... | collective-permute-start | bytes 786440 | tf_op jit(solution)/shard_map/ppermute | solution.py:244
  209.6 9.1 %fusion.5 = f32[64,2,8,8,128]{4,0,1,3,2:T(8,128)S(1)} fusion(f32[64,2,8,8,128]{4,2,3,1,0:T(8,128)S(1)} %bitcast.60, s32[8,8,64]{2,1,0:T(8,128)S(1)} %get-tuple-element.140, s32[8,8,64]{2,1,0:T(8,128)S(1)} %get-tuple-element.141, s32[8,8,64]{2,1,0:T(8,128)S(1)} %get-tuple-element.139, f32[8,8,64]{2,1,0:T(8,128)S(1)} %divide_multiply_fusion), kind=kOutput, calls=%fused_computation.6 | convolution fusion | flops 807927808 | bytes 8454144 | tf_op jit(solution)/shard_map/rbek,kfrbc->efrbc/dot_general | solution.py:227
  221.0 4.3 %collective-permute-start.22 = (f32[8,1,8,1024]{3,1,2,0:T(1,128)}, f32[8,1,8,1024]{3,1,2,0:T(1,128)}, u32[]{:S(2)}, u32[]{:S(2)}) collective-permute-start(f32[8,1,8,1024]{3,1,2,0:T(1,128)} %bitcast.19), channel_id=1, source_target_pairs={{0,28},{4,0},{8,4},{12,8},{16,12},{20,16},{24,20},{28,24},{1,29},{... | collective-permute-start | bytes 786440 | tf_op jit(solution)/shard_map/ppermute | solution.py:244
  231.4 2.0 copy.32
  241.5 6.6 %collective-permute-done.20 = f32[8,1,8,1024]{3,1,2,0:T(1,128)S(1)} collective-permute-done((f32[8,1,8,1024]{3,1,2,0:T(1,128)}, f32[8,1,8,1024]{3,1,2,0:T(1,128)S(1)}, u32[]{:S(2)}, u32[]{:S(2)}) %collective-permute-start.20) | collective-permute-done | bytes 262176 | tf_op jit(solution)/shard_map/ppermute | solution.py:244
  248.1 14.1 %collective-permute-start.39 = (f32[8,2,8,1024]{3,2,1,0:T(8,128)}, f32[8,2,8,1024]{3,2,1,0:T(8,128)}, u32[]{:S(2)}, u32[]{:S(2)}) collective-permute-start(f32[8,2,8,1024]{3,2,1,0:T(8,128)} %slice.139), channel_id=1, source_target_pairs={{0,12},{4,16},{8,20},{12,24},{16,28},{20,0},{24,4},{28,8},{1,13},{... | collective-permute-start | bytes 1572872 | tf_op jit(solution)/shard_map/ppermute | solution.py:244
  264.1 14.2 %collective-permute-start.40 = (f32[8,2,8,1024]{3,2,1,0:T(8,128)}, f32[8,2,8,1024]{3,2,1,0:T(8,128)}, u32[]{:S(2)}, u32[]{:S(2)}) collective-permute-start(f32[8,2,8,1024]{3,2,1,0:T(8,128)} %slice.141), channel_id=1, source_target_pairs={{0,16},{4,20},{8,24},{12,28},{16,0},{20,4},{24,8},{28,12},{1,17},{... | collective-permute-start | bytes 1572872 | tf_op jit(solution)/shard_map/ppermute | solution.py:244
  285.7 2.4 collective-permute-start.43
  291.9 32.5 %collective-permute-done.40 = f32[8,2,8,1024]{3,2,1,0:T(8,128)} collective-permute-done((f32[8,2,8,1024]{3,2,1,0:T(8,128)}, f32[8,2,8,1024]{3,2,1,0:T(8,128)}, u32[]{:S(2)}, u32[]{:S(2)}) %collective-permute-start.40) | collective-permute-done | bytes 524320 | tf_op jit(solution)/shard_map/ppermute | solution.py:244
  326.3 16.5 %collective-permute-done.41 = f32[8,2,8,1024]{3,2,1,0:T(8,128)S(1)} collective-permute-done((f32[8,2,8,1024]{3,2,1,0:T(8,128)S(1)}, f32[8,2,8,1024]{3,2,1,0:T(8,128)S(1)}, u32[]{:S(2)}, u32[]{:S(2)}) %collective-permute-start.41) | collective-permute-done | bytes 524320 | tf_op jit(solution)/shard_map/ppermute | solution.py:244
  (166 shorter events, 79.5 us)
Async XLA Ops:
  1.6 27.3 %collective-permute-start.8 = (f32[8,3,4,1024]{3,2,1,0:T(4,128)S(1)}, f32[8,3,4,1024]{3,2,1,0:T(4,128)S(1)}, u32[]{:S(2)}, u32[]{:S(2)}) collective-permute-start(f32[8,3,4,1024]{3,2,1,0:T(4,128)S(1)} %get-tuple-element.105), channel_id=1, source_target_pairs={{1,0},{2,1},{3,2},{5,4},{6,5},{7,6},{9,8},{10,9},{11,10},{13,12},{... | collective-permute-start | bytes 1179656 | tf_op jit(solution)/shard_map/ppermute | solution.py:32
  2.9 28.7 %collective-permute-start.7 = (f32[8,3,4,1024]{3,2,1,0:T(4,128)S(1)}, f32[8,3,4,1024]{3,2,1,0:T(4,128)S(1)}, u32[]{:S(2)}, u32[]{:S(2)}) collective-permute-start(f32[8,3,4,1024]{3,2,1,0:T(4,128)S(1)} %get-tuple-element.106), channel_id=1, source_target_pairs={{0,1},{1,2},{2,3},{4,5},{5,6},{6,7},{8,9},{9,10},{10,11},{12,13},{... | collective-permute-start | bytes 1179656 | tf_op jit(solution)/shard_map/ppermute | solution.py:31
  17.2 27.5 %collective-permute-start = (f32[8,8,1024]{2,1,0:T(8,128)}, f32[8,8,1024]{2,1,0:T(8,128)S(1)}, u32[]{:S(2)}, u32[]{:S(2)}) collective-permute-start(f32[8,8,1024]{2,1,0:T(8,128)} %get-tuple-element.56), channel_id=1, source_target_pairs={{0,4},{4,8},{8,12},{12,16},{16,20},{20,24},{1,5},{5,9},{9,13},{13,... | collective-permute-start | bytes 786440 | tf_op jit(solution)/shard_map/ppermute | solution.py:244
  17.8 32.9 %collective-permute-start.1 = (f32[8,8,1024]{2,1,0:T(8,128)}, f32[8,8,1024]{2,1,0:T(8,128)}, u32[]{:S(2)}, u32[]{:S(2)}) collective-permute-start(f32[8,8,1024]{2,1,0:T(8,128)} %get-tuple-element.57), channel_id=1, source_target_pairs={{0,8},{4,12},{8,16},{12,20},{16,24},{28,4},{1,9},{5,13},{9,17},{13... | collective-permute-start | bytes 786440 | tf_op jit(solution)/shard_map/ppermute | solution.py:244
  23.4 29.3 %collective-permute-start.2 = (f32[8,8,1024]{2,1,0:T(8,128)}, f32[8,8,1024]{2,1,0:T(8,128)}, u32[]{:S(2)}, u32[]{:S(2)}) collective-permute-start(f32[8,8,1024]{2,1,0:T(8,128)} %get-tuple-element.58), channel_id=1, source_target_pairs={{0,12},{4,16},{8,20},{12,24},{24,4},{28,8},{1,13},{5,17},{9,21},{1... | collective-permute-start | bytes 786440 | tf_op jit(solution)/shard_map/ppermute | solution.py:244
  28.9 25.8 %collective-permute-start.3 = (f32[8,8,1024]{2,1,0:T(8,128)}, f32[8,8,1024]{2,1,0:T(8,128)}, u32[]{:S(2)}, u32[]{:S(2)}) collective-permute-start(f32[8,8,1024]{2,1,0:T(8,128)} %get-tuple-element.59), channel_id=1, source_target_pairs={{0,16},{4,20},{8,24},{20,4},{24,8},{28,12},{1,17},{5,21},{9,25},{2... | collective-permute-start | bytes 786440 | tf_op jit(solution)/shard_map/ppermute | solution.py:244
  61.1 27.0 %collective-permute-start.13 = (f32[8,8,1024]{2,1,0:T(8,128)S(1)}, f32[8,8,1024]{2,1,0:T(8,128)S(1)}, u32[]{:S(2)}, u32[]{:S(2)}) collective-permute-start(f32[8,8,1024]{2,1,0:T(8,128)S(1)} %get-tuple-element.69), channel_id=1, source_target_pairs={{8,28},{12,0},{9,29},{13,1},{10,30},{14,2},{11,31},{15,3}} | collective-permute-start | bytes 786440 | tf_op jit(solution)/shard_map/ppermute | solution.py:244
  79.7 40.9 %collective-permute-start.24 = (f32[8,2,8,1024]{3,2,1,0:T(8,128)S(1)}, f32[8,2,8,1024]{3,2,1,0:T(8,128)S(1)}, u32[]{:S(2)}, u32[]{:S(2)}) collective-permute-start(f32[8,2,8,1024]{3,2,1,0:T(8,128)S(1)} %copy-done.13), channel_id=1, source_target_pairs={{0,4},{4,8},{8,12},{12,16},{16,20},{20,24},{1,5},{5,9},{9,13},{13,... | collective-permute-start | bytes 1572872 | tf_op jit(solution)/shard_map/ppermute | solution.py:244
  80.4 42.9 %collective-permute-start.26 = (f32[8,2,8,1024]{3,2,1,0:T(8,128)S(1)}, f32[8,2,8,1024]{3,2,1,0:T(8,128)S(1)}, u32[]{:S(2)}, u32[]{:S(2)}) collective-permute-start(f32[8,2,8,1024]{3,2,1,0:T(8,128)S(1)} %copy-done.12), channel_id=1, source_target_pairs={{0,8},{4,12},{8,16},{12,20},{16,24},{28,4},{1,9},{5,13},{9,17},{13... | collective-permute-start | bytes 1572872 | tf_op jit(solution)/shard_map/ppermute | solution.py:244
  88.1 42.1 %collective-permute-start.28 = (f32[8,2,8,1024]{3,2,1,0:T(8,128)S(1)}, f32[8,2,8,1024]{3,2,1,0:T(8,128)S(1)}, u32[]{:S(2)}, u32[]{:S(2)}) collective-permute-start(f32[8,2,8,1024]{3,2,1,0:T(8,128)S(1)} %copy-done.11), channel_id=1, source_target_pairs={{0,12},{4,16},{8,20},{12,24},{24,4},{28,8},{1,13},{5,17},{9,21},{1... | collective-permute-start | bytes 1572872 | tf_op jit(solution)/shard_map/ppermute | solution.py:244
  89.9 32.0 %collective-permute-start.23 = (f32[8,2,8,1024]{3,2,1,0:T(8,128)S(1)}, f32[8,2,8,1024]{3,2,1,0:T(8,128)S(1)}, u32[]{:S(2)}, u32[]{:S(2)}) collective-permute-start(f32[8,2,8,1024]{3,2,1,0:T(8,128)S(1)} %get-tuple-element.91), channel_id=1, source_target_pairs={{24,28},{28,0},{25,29},{29,1},{26,30},{30,2},{27,31},{31,3}} | collective-permute-start | bytes 1572872 | tf_op jit(solution)/shard_map/ppermute | solution.py:244
  92.2 36.6 %collective-permute-start.25 = (f32[8,2,8,1024]{3,2,1,0:T(8,128)S(1)}, f32[8,2,8,1024]{3,2,1,0:T(8,128)S(1)}, u32[]{:S(2)}, u32[]{:S(2)}) collective-permute-start(f32[8,2,8,1024]{3,2,1,0:T(8,128)S(1)} %get-tuple-element.93), channel_id=1, source_target_pairs={{20,28},{24,0},{21,29},{25,1},{22,30},{26,2},{23,31},{27,3}} | collective-permute-start | bytes 1572872 | tf_op jit(solution)/shard_map/ppermute | solution.py:244
  123.3 46.6 %collective-permute-start.32 = (f32[8,2,8,1024]{3,2,1,0:T(8,128)S(1)}, f32[8,2,8,1024]{3,2,1,0:T(8,128)S(1)}, u32[]{:S(2)}, u32[]{:S(2)}) collective-permute-start(f32[8,2,8,1024]{3,2,1,0:T(8,128)S(1)} %copy-done.9), channel_id=1, source_target_pairs={{0,20},{4,24},{16,4},{20,8},{24,12},{28,16},{1,21},{5,25},{17,5},{... | collective-permute-start | bytes 1572872 | tf_op jit(solution)/shard_map/ppermute | solution.py:244
  128.8 39.7 %collective-permute-start.29 = (f32[8,2,8,1024]{3,2,1,0:T(8,128)S(1)}, f32[8,2,8,1024]{3,2,1,0:T(8,128)S(1)}, u32[]{:S(2)}, u32[]{:S(2)}) collective-permute-start(f32[8,2,8,1024]{3,2,1,0:T(8,128)S(1)} %get-tuple-element.97), channel_id=1, source_target_pairs={{12,28},{16,0},{13,29},{17,1},{14,30},{18,2},{15,31},{19,3}} | collective-permute-start | bytes 1572872 | tf_op jit(solution)/shard_map/ppermute | solution.py:244
  130.2 51.7 %collective-permute-start.34 = (f32[8,2,8,1024]{3,2,1,0:T(8,128)S(1)}, f32[8,2,8,1024]{3,2,1,0:T(8,128)S(1)}, u32[]{:S(2)}, u32[]{:S(2)}) collective-permute-start(f32[8,2,8,1024]{3,2,1,0:T(8,128)S(1)} %copy-done.8), channel_id=1, source_target_pairs={{0,24},{12,4},{16,8},{20,12},{24,16},{28,20},{1,25},{13,5},{17,9},... | collective-permute-start | bytes 1572872 | tf_op jit(solution)/shard_map/ppermute | solution.py:244
  139.4 37.8 %collective-permute-start.31 = (f32[8,2,8,1024]{3,2,1,0:T(8,128)S(1)}, f32[8,2,8,1024]{3,2,1,0:T(8,128)S(1)}, u32[]{:S(2)}, u32[]{:S(2)}) collective-permute-start(f32[8,2,8,1024]{3,2,1,0:T(8,128)S(1)} %get-tuple-element.99), channel_id=1, source_target_pairs={{8,28},{12,0},{9,29},{13,1},{10,30},{14,2},{11,31},{15,3}} | collective-permute-start | bytes 1572872 | tf_op jit(solution)/shard_map/ppermute | solution.py:244
  140.8 66.2 %collective-permute-start.36 = (f32[8,2,8,1024]{3,2,1,0:T(8,128)S(1)}, f32[8,2,8,1024]{3,2,1,0:T(8,128)S(1)}, u32[]{:S(2)}, u32[]{:S(2)}) collective-permute-start(f32[8,2,8,1024]{3,2,1,0:T(8,128)S(1)} %copy-done.7), channel_id=1, source_target_pairs={{8,4},{12,8},{16,12},{20,16},{24,20},{28,24},{9,5},{13,9},{17,13},... | collective-permute-start | bytes 1572872 | tf_op jit(solution)/shard_map/ppermute | solution.py:244
  169.9 38.0 %collective-permute-start.35 = (f32[8,2,8,1024]{3,2,1,0:T(8,128)S(1)}, f32[8,2,8,1024]{3,2,1,0:T(8,128)S(1)}, u32[]{:S(2)}, u32[]{:S(2)}) collective-permute-start(f32[8,2,8,1024]{3,2,1,0:T(8,128)S(1)} %get-tuple-element.103), channel_id=1, source_target_pairs={{0,28},{4,0},{1,29},{5,1},{2,30},{6,2},{3,31},{7,3}} | collective-permute-start | bytes 1572872 | tf_op jit(solution)/shard_map/ppermute | solution.py:244
  177.2 43.0 %collective-permute-start.16 = (f32[8,1,8,1024]{3,1,2,0:T(1,128)S(1)}, f32[8,1,8,1024]{3,1,2,0:T(1,128)S(1)}, u32[]{:S(2)}, u32[]{:S(2)}) collective-permute-start(f32[8,1,8,1024]{3,1,2,0:T(1,128)S(1)} %bitcast.59), channel_id=1, source_target_pairs={{0,4},{4,8},{8,12},{12,16},{16,20},{20,24},{24,28},{28,0},{1,5},{5... | collective-permute-start | bytes 786440 | tf_op jit(solution)/shard_map/ppermute | solution.py:244
  181.9 39.0 %collective-permute-start.17 = (f32[8,1,8,1024]{3,1,2,0:T(1,128)S(1)}, f32[8,1,8,1024]{3,1,2,0:T(1,128)S(1)}, u32[]{:S(2)}, u32[]{:S(2)}) collective-permute-start(f32[8,1,8,1024]{3,1,2,0:T(1,128)S(1)} %bitcast.58), channel_id=1, source_target_pairs={{0,8},{4,12},{8,16},{12,20},{16,24},{20,28},{24,0},{28,4},{1,9},{5... | collective-permute-start | bytes 786440 | tf_op jit(solution)/shard_map/ppermute | solution.py:244
  187.1 41.8 %collective-permute-start.18 = (f32[8,1,8,1024]{3,1,2,0:T(1,128)}, f32[8,1,8,1024]{3,1,2,0:T(1,128)}, u32[]{:S(2)}, u32[]{:S(2)}) collective-permute-start(f32[8,1,8,1024]{3,1,2,0:T(1,128)} %bitcast.15), channel_id=1, source_target_pairs={{0,12},{4,16},{8,20},{12,24},{16,28},{20,0},{24,4},{28,8},{1,13},{... | collective-permute-start | bytes 786440 | tf_op jit(solution)/shard_map/ppermute | solution.py:244
  207.0 28.4 %collective-permute-start.19 = (f32[8,1,8,1024]{3,1,2,0:T(1,128)}, f32[8,1,8,1024]{3,1,2,0:T(1,128)}, u32[]{:S(2)}, u32[]{:S(2)}) collective-permute-start(f32[8,1,8,1024]{3,1,2,0:T(1,128)} %bitcast.16), channel_id=1, source_target_pairs={{0,16},{4,20},{8,24},{12,28},{16,0},{20,4},{24,8},{28,12},{1,17},{... | collective-permute-start | bytes 786440 | tf_op jit(solution)/shard_map/ppermute | solution.py:244
  208.0 40.2 %collective-permute-start.20 = (f32[8,1,8,1024]{3,1,2,0:T(1,128)}, f32[8,1,8,1024]{3,1,2,0:T(1,128)S(1)}, u32[]{:S(2)}, u32[]{:S(2)}) collective-permute-start(f32[8,1,8,1024]{3,1,2,0:T(1,128)} %bitcast.17), channel_id=1, source_target_pairs={{0,20},{4,24},{8,28},{12,0},{16,4},{20,8},{24,12},{28,16},{1,21},{... | collective-permute-start | bytes 786440 | tf_op jit(solution)/shard_map/ppermute | solution.py:244
  220.1 44.0 %collective-permute-start.21 = (f32[8,1,8,1024]{3,1,2,0:T(1,128)}, f32[8,1,8,1024]{3,1,2,0:T(1,128)}, u32[]{:S(2)}, u32[]{:S(2)}) collective-permute-start(f32[8,1,8,1024]{3,1,2,0:T(1,128)} %bitcast.18), channel_id=1, source_target_pairs={{0,24},{4,28},{8,0},{12,4},{16,8},{20,12},{24,16},{28,20},{1,25},{... | collective-permute-start | bytes 786440 | tf_op jit(solution)/shard_map/ppermute | solution.py:244
  221.0 59.6 %collective-permute-start.22 = (f32[8,1,8,1024]{3,1,2,0:T(1,128)}, f32[8,1,8,1024]{3,1,2,0:T(1,128)}, u32[]{:S(2)}, u32[]{:S(2)}) collective-permute-start(f32[8,1,8,1024]{3,1,2,0:T(1,128)} %bitcast.19), channel_id=1, source_target_pairs={{0,28},{4,0},{8,4},{12,8},{16,12},{20,16},{24,20},{28,24},{1,29},{... | collective-permute-start | bytes 786440 | tf_op jit(solution)/shard_map/ppermute | solution.py:244
  228.9 54.8 %collective-permute-start.37 = (f32[8,2,8,1024]{3,2,1,0:T(8,128)}, f32[8,2,8,1024]{3,2,1,0:T(8,128)}, u32[]{:S(2)}, u32[]{:S(2)}) collective-permute-start(f32[8,2,8,1024]{3,2,1,0:T(8,128)} %slice.135), channel_id=1, source_target_pairs={{0,4},{4,8},{8,12},{12,16},{16,20},{20,24},{24,28},{28,0},{1,5},{5... | collective-permute-start | bytes 1572872 | tf_op jit(solution)/shard_map/ppermute | solution.py:244
  235.4 50.3 %collective-permute-start.38 = (f32[8,2,8,1024]{3,2,1,0:T(8,128)}, f32[8,2,8,1024]{3,2,1,0:T(8,128)}, u32[]{:S(2)}, u32[]{:S(2)}) collective-permute-start(f32[8,2,8,1024]{3,2,1,0:T(8,128)} %slice.137), channel_id=1, source_target_pairs={{0,8},{4,12},{8,16},{12,20},{16,24},{20,28},{24,0},{28,4},{1,9},{5... | collective-permute-start | bytes 1572872 | tf_op jit(solution)/shard_map/ppermute | solution.py:244
  248.1 41.9 %collective-permute-start.39 = (f32[8,2,8,1024]{3,2,1,0:T(8,128)}, f32[8,2,8,1024]{3,2,1,0:T(8,128)}, u32[]{:S(2)}, u32[]{:S(2)}) collective-permute-start(f32[8,2,8,1024]{3,2,1,0:T(8,128)} %slice.139), channel_id=1, source_target_pairs={{0,12},{4,16},{8,20},{12,24},{16,28},{20,0},{24,4},{28,8},{1,13},{... | collective-permute-start | bytes 1572872 | tf_op jit(solution)/shard_map/ppermute | solution.py:244
  264.1 60.3 %collective-permute-start.40 = (f32[8,2,8,1024]{3,2,1,0:T(8,128)}, f32[8,2,8,1024]{3,2,1,0:T(8,128)}, u32[]{:S(2)}, u32[]{:S(2)}) collective-permute-start(f32[8,2,8,1024]{3,2,1,0:T(8,128)} %slice.141), channel_id=1, source_target_pairs={{0,16},{4,20},{8,24},{12,28},{16,0},{20,4},{24,8},{28,12},{1,17},{... | collective-permute-start | bytes 1572872 | tf_op jit(solution)/shard_map/ppermute | solution.py:244
  280.6 62.3 %collective-permute-start.41 = (f32[8,2,8,1024]{3,2,1,0:T(8,128)S(1)}, f32[8,2,8,1024]{3,2,1,0:T(8,128)S(1)}, u32[]{:S(2)}, u32[]{:S(2)}) collective-permute-start(f32[8,2,8,1024]{3,2,1,0:T(8,128)S(1)} %slice.143), channel_id=1, source_target_pairs={{0,20},{4,24},{8,28},{12,0},{16,4},{20,8},{24,12},{28,16},{1,21},{... | collective-permute-start | bytes 1572872 | tf_op jit(solution)/shard_map/ppermute | solution.py:244
  283.7 59.9 %collective-permute-start.42 = (f32[8,2,8,1024]{3,2,1,0:T(8,128)S(1)}, f32[8,2,8,1024]{3,2,1,0:T(8,128)S(1)}, u32[]{:S(2)}, u32[]{:S(2)}) collective-permute-start(f32[8,2,8,1024]{3,2,1,0:T(8,128)S(1)} %slice.145), channel_id=1, source_target_pairs={{0,24},{4,28},{8,0},{12,4},{16,8},{20,12},{24,16},{28,20},{1,25},{... | collective-permute-start | bytes 1572872 | tf_op jit(solution)/shard_map/ppermute | solution.py:244
  285.7 58.8 %collective-permute-start.43 = (f32[8,2,8,1024]{3,2,1,0:T(8,128)S(1)}, f32[8,2,8,1024]{3,2,1,0:T(8,128)S(1)}, u32[]{:S(2)}, u32[]{:S(2)}) collective-permute-start(f32[8,2,8,1024]{3,2,1,0:T(8,128)S(1)} %slice.147), channel_id=1, source_target_pairs={{0,28},{4,0},{8,4},{12,8},{16,12},{20,16},{24,20},{28,24},{1,29},{... | collective-permute-start | bytes 1572872 | tf_op jit(solution)/shard_map/ppermute | solution.py:244
  (27 other events, 519.7 us)
